TPU v7x, 512 devices: a 8x2x16 block of a 8x8x16 slice. The times are simulated.
512 devices in a mesh: groups: 2 (over y), seq: 16 (over z), heads: 8 (over x), sub: 2 (over core).
Axes of the slice: x: 8, y: 2, z: 16, core: 2. Of those that a mesh axis runs over, the one named last changes fastest.
The devices are a block of a 8x8x16 slice.
Arguments:
- queries: bfloat16 [8192, 8192], P(('groups', 'seq', 'sub'), 'heads'), parts along dimension 0, may hold values from -400 to 400
- keys: bfloat16 [8192, 1024], P(('groups', 'seq', 'sub'), 'heads'), parts along dimension 0, may hold values from -6 to 6
- values: bfloat16 [8192, 1024], P(('groups', 'seq', 'sub'), 'heads'), parts along dimension 0, may hold values from -18 to 18
- half_order: int32 [128], P('groups'), parts along dimension 0, may hold values from 0 to 63, as said below
- frame_lengths: int32 [64], P('groups'), parts along dimension 0, may hold values from 1 to 256, 4096 in all
- out_proj: bfloat16 [8192, 4096], P('heads', ('seq', 'sub')), may hold values from -0.125 to 0.125
- residual_in: bfloat16 [8192, 4096], P(('groups', 'seq', 'sub'), 'heads'), parts along dimension 0, may hold values from -40 to 40
- norm_gain: float32 [4096], P('heads'), may hold values from 0.5 to 1.5
Outputs:
- attended: bfloat16 [8192, 8192], P(('groups', 'seq', 'sub'), 'heads'), parts along dimension 0
- hidden_state: bfloat16 [8192, 4096], P(('groups', 'seq', 'sub'), 'heads'), parts along dimension 0
- normed: bfloat16 [8192, 4096], P(('groups', 'seq', 'sub'), 'heads'), parts along dimension 0
There are 2 independent parts, one for each index of `groups`. A program takes and returns all parts, laid end to end along the dimension named above; an argument that names none is the same for every part. Nothing has to cross between parts.
Inputs may be any that keep to these rules, and one draw needn't show every extreme that they name: `half_order`: a permutation of 0 to 63.
All inputs are finite; a program needn't handle non-finite values.
Results may differ from a plain program's by a relative error of at most 0.005.
Values may be sent and summed in bfloat16 or wider, within the bound.
A program may use at most 64 MiB of HBM per device.

v0:
```python
import jax
import jax.numpy as jnp
from jax import lax
from jax.sharding import PartitionSpec as P

HEAD_WIDTH = 128
OUT_WIDTH = 4096


def side_by_side(arrays, axis, dim, along):
    ends, at = ([], 0)
    for a in arrays[:-1]:
        at += a.shape[along]
        ends.append(at)
    both = jnp.concatenate(arrays, axis=along)
    return tuple(jnp.split(lax.all_gather(both, axis, axis=dim, tiled=True), ends, axis=along))


def split_up(value, dim, devices):
    shape = value.shape
    parts = value.reshape(*shape[:dim], devices, shape[dim] // devices, *shape[dim + 1 :])
    return jnp.moveaxis(parts, dim, 0)


def summed_on_arrival(value, axis, dim):
    devices = lax.axis_size(axis)
    parts = lax.all_to_all(split_up(value, dim, devices), axis, 0, 0, tiled=True)
    return jnp.sum(parts.astype(jnp.float32), axis=0)


def from_everyone(value, axis):
    copies = jnp.broadcast_to(value, (lax.axis_size(axis), *value.shape))
    return lax.all_to_all(copies, axis, split_axis=0, concat_axis=0, tiled=True)


def of_everyone(value, axis):
    return from_everyone(value, axis).sum(axis=0)


def shards(queries, keys, values, half_order, frame_lengths, out_proj, residual_in, norm_gain):
    tok_rows = queries.shape[0]
    kv_local = keys.shape[1] // HEAD_WIDTH
    group_width = queries.shape[1] // keys.shape[1]
    half_rows = tok_rows // 2
    own_index = lax.axis_index("seq") * lax.axis_size("sub") + lax.axis_index("sub")
    table_ids = jnp.arange(half_order.shape[0], dtype=jnp.int32)

    def locate(row_ids):
        matches = (row_ids // half_rows)[:, None] == table_ids[None, :]
        offsets = jnp.sum(jnp.where(matches, half_order[None, :], 0), axis=1)
        return offsets * half_rows + row_ids % half_rows

    query_pos = locate(own_index * tok_rows + jnp.arange(tok_rows, dtype=jnp.int32))
    frame_ends = jnp.cumsum(frame_lengths)
    frame_starts = frame_ends - frame_lengths
    frame_limit = jnp.sum(
        jnp.where(frame_starts[None, :] <= query_pos[:, None], frame_lengths[None, :], 0), axis=1
    )
    query_head_rows = queries.reshape(tok_rows, kv_local, group_width, HEAD_WIDTH)
    score_scale = HEAD_WIDTH ** (-0.5)
    initial = (
        jnp.full((kv_local, group_width, tok_rows), -1e30, jnp.float32),
        jnp.zeros((kv_local, group_width, tok_rows), jnp.float32),
        jnp.zeros((kv_local, group_width, tok_rows, HEAD_WIDTH), jnp.float32),
    )
    key_piece, value_piece = side_by_side((keys, values), ("seq", "sub"), 0, 1)
    piece_rows = key_piece.shape[0]
    key_pos = locate(jnp.arange(piece_rows, dtype=jnp.int32))

    def absorb_piece(current):
        running_max, denominator, numerator = current
        key_view = key_piece.reshape(piece_rows, kv_local, HEAD_WIDTH)
        value_view = value_piece.reshape(piece_rows, kv_local, HEAD_WIDTH)
        scores = (
            jnp.einsum(
                "qhgd,khd->hgqk", query_head_rows, key_view, preferred_element_type=jnp.float32
            )
            * score_scale
        )
        visible = key_pos[None, :] < frame_limit[:, None]
        scores = jnp.where(visible, scores, -1e30)
        new_max = jnp.maximum(running_max, jnp.max(scores, axis=-1))
        weights = jnp.where(visible, jnp.exp(scores - new_max[..., None]), 0.0)
        denominator = jnp.sum(weights, axis=-1)
        product = jnp.einsum(
            "hgqk,khd->hgqd",
            weights.astype(jnp.bfloat16),
            value_view,
            preferred_element_type=jnp.float32,
        )
        numerator = product
        return (new_max, denominator, numerator)

    running_max, denominator, numerator = lax.cond(
        jnp.min(key_pos) < jnp.max(frame_limit), absorb_piece, lambda current: current, initial
    )
    result = numerator / denominator[..., None]
    attended = (
        jnp.transpose(result, (2, 0, 1, 3))
        .reshape(tok_rows, kv_local * group_width * HEAD_WIDTH)
        .astype(jnp.bfloat16)
    )
    head_terms = jnp.dot(
        attended,
        lax.all_gather(out_proj, ("seq", "sub"), axis=1, tiled=True),
        preferred_element_type=jnp.float32,
    )
    projected = summed_on_arrival(head_terms.astype(jnp.bfloat16), "heads", 1)
    hidden_state = (residual_in.astype(jnp.float32) + projected).astype(jnp.bfloat16)
    widened = hidden_state.astype(jnp.float32)
    energy = of_everyone(jnp.sum(widened * widened, axis=1), "heads") / OUT_WIDTH
    normed = (widened * lax.rsqrt(energy + 1e-06)[:, None] * norm_gain[None, :]).astype(
        jnp.bfloat16
    )
    return (attended, hidden_state, normed)


def solution(mesh):
    in_specs = (
        P(("groups", "seq", "sub"), "heads"),
        P(("groups", "seq", "sub"), "heads"),
        P(("groups", "seq", "sub"), "heads"),
        P("groups"),
        P("groups"),
        P("heads", ("seq", "sub")),
        P(("groups", "seq", "sub"), "heads"),
        P("heads"),
    )
    out_specs = (
        P(("groups", "seq", "sub"), "heads"),
        P(("groups", "seq", "sub"), "heads"),
        P(("groups", "seq", "sub"), "heads"),
    )
    return jax.shard_map(shards, mesh=mesh, in_specs=in_specs, out_specs=out_specs, check_vma=False)
```

profile of v0, /device:TPU:65, one launch (start us, length us, event | category | flops | bytes accessed | tf_op | source)
XLA Modules:
  0.0 272.1 jit_solution(6806642003269453513)
XLA Ops:
  7.2 0.1 all-gather.3.cloned.1.call-start
  7.2 1.4 pad_maximum_fusion
  8.7 0.1 all-gather.3.cloned.1.call-update
  8.7 0.1 all-gather.5.cloned.1.call-start
  8.8 0.7 all-gather.5.cloned.1.call-update
  9.5 0.7 copy.32
  10.3 0.1 reduce-window.9
  10.3 0.1 reduce.3
  10.5 0.7 sub.24
  11.1 0.7 select_reduce_fusion.1
  11.9 0.7 select_reduce_fusion.2
  12.6 0.6 reduce_max.18
  13.3 0.9 select_reduce_fusion
  14.2 0.6 fusion.33
  16.1 103.1 %all-gather.3.cloned.1.call-done = bf16[4096,256]{1,0:T(8,128)(2,1)} async-done(((bf16[128,256]{1,0:T(8,128)(2,1)}), bf16[4096,256]{1,0:T(8,128)(2,1)}) %all-gather.3.cloned.1.call-update) | async-done | bytes 2097168 | tf_op jit(solution)/shard_map/all_gather | solution.py:16
  119.3 14.2 %conditional.1 = (f32[1,8,128]{2,1,0:T(8,128)S(1)}, f32[1,8,128,128]{3,2,1,0:T(8,128)S(1)}) conditional(s32[]{:T(128)} %convert_element_type.33, () %tuple.16, (s32[4096]{0:T(1024)S(1)}, s32[128]{0:T(128)S(1)}, bf16[4096,256]{1,0:T(8,128)(2,1)}, bf16[128,1024]{1,0:T(8,128)(2,1)}) %tuple.17), branch_computations={%region_6.7_spmd, %region_7.10_spmd} | conditional | flops 2202532864 | bytes 63742508 | solution.py:94
  119.3 1.8 broadcast_compare_fusion
  121.1 3.8 %fusion = (f32[8,128]{1,0:T(8,128)S(1)}, f32[4096,128,8]{1,0,2:T(8,128)S(1)}) fusion(pred[128,4096]{0,1:T(8,128)(4,1)S(1)} %broadcast_compare_fusion, bf16[4096,256]{1,0:T(8,128)(2,1)} %get-tuple-element.14, bf16[128,1024]{1,0:T(8,128)(2,1)} %get-tuple-element.24), kind=kOutput, calls=%fused_computation.2 | convolution fusion | flops 1086323712 | bytes 18616320 | tf_op jit(solution)/shard_map/cond/branch_1_fun/qhgd,khd->hgqk/dot_general | solution.py:75
  124.9 4.4 %fusion.7 = f32[1,8,128,128]{3,2,1,0:T(8,128)S(1)} fusion(f32[4096,128,8]{1,0,2:T(8,128)S(1)} %get-tuple-element.30, f32[8,128]{1,0:T(8,128)S(1)} %broadcast_maximum_fusion, pred[128,4096]{0,1:T(8,128)(4,1)S(1)} %broadcast_compare_fusion, bf16[4096,256]{1,0:T(8,128)(2,1)S(1)} %copy-done.4), kind=kOutput, calls=%fused_computation.8 | convolution fusion | flops 1094713344 | bytes 18878464 | tf_op jit(solution)/shard_map/cond/branch_1_fun/hgqk,khd->hgqd/dot_general | solution.py:85
  129.4 4.0 %fusion.2 = f32[8,128]{1,0:T(8,128)S(1)} fusion(f32[4096,128,8]{1,0,2:T(8,128)S(1)} %get-tuple-element.30, f32[8,128]{1,0:T(8,128)S(1)} %broadcast_maximum_fusion, pred[128,4096]{0,1:T(8,128)(4,1)S(1)} %broadcast_compare_fusion), kind=kLoop, calls=%fused_computation.4 | loop fusion | flops 20970496 | bytes 17309696 | tf_op jit(solution)/shard_map/cond/branch_1_fun/reduce_sum | solution.py:84
  133.4 0.0 copy-start.2
  133.4 0.0 copy-start.3
  133.4 0.2 fusion.23
  133.7 0.2 copy.33
  133.9 81.7 %all-gather.5.cloned.1.call-done = bf16[1024,4096]{1,0:T(8,128)(2,1)} async-done(((bf16[1024,128]{1,0:T(8,128)(2,1)}), bf16[1024,4096]{1,0:T(8,128)(2,1)}) %all-gather.5.cloned.1.call-update) | async-done | bytes 8388624 | tf_op jit(solution)/shard_map/all_gather | solution.py:105
  215.6 4.6 %convolution_convert_fusion = bf16[128,4096]{1,0:T(8,128)(2,1)S(1)} fusion(bf16[128,1024]{1,0:T(8,128)(2,1)S(1)} %bitcast.64, bf16[1024,4096]{1,0:T(8,128)(2,1)} %all-gather.5.cloned.1.call-done), kind=kOutput, calls=%fused_computation.21 | convolution fusion | flops 1074266112 | bytes 9699328 | tf_op jit(solution)/shard_map/dot_general | solution.py:103
  220.3 0.1 copy.48
  220.3 34.8 %all_to_all.11 = bf16[8,128,512]{2,1,0:T(8,128)(2,1)S(1)} all-to-all(bf16[8,128,512]{2,1,0:T(8,128)(2,1)S(1)} %bitcast.62), channel_id=1, replica_groups=mesh['groups'=2,'seq'=16,'heads'=8,'sub'=2] {'heads'}, dimensions={0} | all-to-all | bytes 2097152 | tf_op jit(solution)/shard_map/all_to_all | solution.py:27
  255.2 0.1 convert_reduce_fusion
  255.3 0.1 fusion.20
  255.5 9.0 %all_to_all.12 = f32[8,1,128]{2,1,0:T(1,128)S(1)} all-to-all(f32[8,1,128]{2,1,0:T(1,128)S(1)} %broadcast_in_dim.81), channel_id=1, replica_groups=mesh['groups'=2,'seq'=16,'heads'=8,'sub'=2] {'heads'}, dimensions={0} | all-to-all | bytes 8192 | tf_op jit(solution)/shard_map/all_to_all | solution.py:33
  264.5 0.8 fusion.22
  (16 shorter events, 0.1 us)
Async XLA Ops:
  7.2 112.1 %all-gather.3.cloned.1.call-start = ((), (), s32[]{:S(2)}) async-start(), calls=%async_computation.2 | async-start | bytes 2162688 | tf_op jit(solution)/shard_map/all_gather | solution.py:16
  8.7 206.9 %all-gather.5.cloned.1.call-start = ((), (), s32[]{:S(2)}) async-start(), calls=%async_computation.3 | async-start | bytes 8650752 | tf_op jit(solution)/shard_map/all_gather | solution.py:105
  119.3 5.7 %copy-start.4 = (bf16[4096,256]{1,0:T(8,128)(2,1)S(1)}, bf16[4096,256]{1,0:T(8,128)(2,1)}, u32[]{:S(2)}) copy-start(bf16[4096,256]{1,0:T(8,128)(2,1)} %get-tuple-element.14) | copy-start | bytes 6291460 | tf_op jit(solution)/shard_map/cond
  133.4 121.9 %copy-start.2 = (bf16[128,512]{1,0:T(8,128)(2,1)S(1)}, bf16[128,512]{1,0:T(8,128)(2,1)}, u32[]{:S(2)}) copy-start(bf16[128,512]{1,0:T(8,128)(2,1)} %param.16) | copy-start | bytes 393220
  133.4 131.0 %copy-start.3 = (f32[512]{0:T(512)S(1)}, f32[512]{0:T(512)}, u32[]{:S(2)}) copy-start(f32[512]{0:T(512)} %param.17) | copy-start | bytes 6148
  133.9 131.3 %copy-start = (bf16[16,8,8,128]{3,1,2,0:T(8,128)(2,1)}, bf16[16,8,8,128]{3,1,2,0:T(8,128)(2,1)S(1)}, u32[]{:S(2)}) copy-start(bf16[16,8,8,128]{3,1,2,0:T(8,128)(2,1)S(1)} %copy.49) | copy-start | bytes 786436
  255.4 9.8 %copy-start.1 = (bf16[128,512]{1,0:T(8,128)(2,1)}, bf16[128,512]{1,0:T(8,128)(2,1)S(1)}, u32[]{:S(2)}) copy-start(bf16[128,512]{1,0:T(8,128)(2,1)S(1)} %get-tuple-element.26) | copy-start | bytes 393220
Sparse Core Ops, SparseCore 0:
  10.7 108.4 all-gather.2
  121.3 94.2 all-gather.4
where the time goes:
time: 272 us
  waiting for transfers between devices  186 us (68%)
  blocking collectives  43.8 us (16%)
  between operations  15.5 us (6%)
  other arithmetic  13.1 us (5%)
  matrix products  12.9 us (5%)
    all_gather x1, waiting for transfers between devices, side_by_side(): lax.all_gather(both, axis, axis=dim, tiled=True)  103 us
    all_gather x1, waiting for transfers between devices, shards(): lax.all_gather(out_proj, ('seq', 'sub'), axis=1, tiled=True)  81.7 us
    all_to_all x1, blocking collectives, summed_on_arrival(): lax.all_to_all(split_up(value, dim, devices), axis, 0, 0, tiled=True)  34.8 us
    all_to_all x1, blocking collectives, from_everyone(): return lax.all_to_all(copies, axis, split_axis=0, concat_axis=0, tiled=True)  8.97 us
  transfers between devices with their start and end apart: 2, of which 2 were waited for; matrix products, arithmetic and copies ran while one was open for 7% of the time, Pallas kernels for 0%

commit v1 on v0

v1 whole, which is shorter than its diff:
```python
import functools

import jax
import jax.numpy as jnp
from jax import lax
from jax.experimental import pallas as pl
from jax.experimental.pallas import tpu as pltpu
from jax.sharding import PartitionSpec as P

HEAD_WIDTH = 128
MASKED = -1e30
SCALE_LOG2 = HEAD_WIDTH ** (-0.5) * 1.4426950408889634
MESH = pl.DeviceIdType.MESH
ROW_TILE = 256


def fused(
    sizes,
    half_ref,
    frame_ref,
    q_hbm,
    k_hbm,
    v_hbm,
    w_hbm,
    res_hbm,
    gain_hbm,
    att_hbm,
    hid_hbm,
    norm_hbm,
    q_buf,
    qaug,
    kv,
    kaug,
    vaug,
    m_buf,
    acc,
    attf,
    wbuf,
    c_out,
    c_in,
    res_buf,
    gain_buf,
    hid_buf,
    norm_buf,
    e_out,
    e_in,
    io_sem,
    kz_s,
    kz_r,
    ks_s,
    ks_r,
    wz_s,
    w_r,
    wy_s,
    c_s,
    c_r,
    a_s,
    a_r,
    e_s,
    e_r,
):
    G, S, H, C = sizes
    use_y = G % 2 == 0
    half = S // 2
    per = S // H
    T = q_buf.shape[0]
    K = wbuf.shape[1]
    heads = q_buf.shape[1] // HEAD_WIDTH
    hb = T // 2
    g, s, h, c = (lax.axis_index(a) for a in ("groups", "seq", "heads", "sub"))
    right, left = lax.rem(s + 1, S), lax.rem(s + S - 1, S)
    other = 1 - c

    ins = [
        pltpu.make_async_copy(k_hbm, kv.at[0, 0, 0], io_sem.at[0]),
        pltpu.make_async_copy(v_hbm, kv.at[0, 0, 1], io_sem.at[1]),
        pltpu.make_async_copy(q_hbm, q_buf, io_sem.at[2]),
        pltpu.make_async_copy(w_hbm, wbuf.at[0], io_sem.at[3]),
        pltpu.make_async_copy(res_hbm, res_buf, io_sem.at[4]),
        pltpu.make_async_copy(gain_hbm, gain_buf, io_sem.at[5]),
    ]
    for copy in ins:
        copy.start()

    barrier = pltpu.get_barrier_semaphore()
    peers = [{"seq": left}, {"seq": right}, {"sub": other}]
    if use_y:
        parity = lax.rem(g, 2)
        partner = g + 1 - 2 * parity
        peers.append({"groups": partner})
    for i in range(1, H):
        to = lax.rem(h + i, H)
        peers.append({"heads": to})
        peers.append({"heads": to, "sub": other})
    for peer in peers:
        pl.semaphore_signal(barrier, inc=1, device_id=peer, device_id_type=MESH)

    if use_y:
        part = K * 5 // 16
        first = pl.ds(pl.multiple_of(parity * (K - part), 16), part)
        second = pl.ds(part, K - 2 * part)
        third = pl.ds(pl.multiple_of((1 - parity) * (K - part), 16), part)
        first_at = pl.multiple_of(parity * (K - part), 16)
    else:
        part = K // 2
        first = pl.ds(0, part)
        second = pl.ds(part, K - part)
        third = None
        first_at = 0
    second_rows = K - 2 * part if use_y else K - part
    pieces = half // 2

    def remote(src, dst, send, recv, device):
        return pltpu.make_async_remote_copy(
            src_ref=src, dst_ref=dst, send_sem=send, recv_sem=recv, device_id=device, device_id_type=MESH
        )

    def got(ref, sem):
        remote(ref, ref, a_s, sem, {"sub": other}).wait_recv()

    def sent(ref, sem):
        remote(ref, ref, sem, a_r, {"sub": other}).wait_send()

    def key_right(d, i):
        remote(kv.at[0, d, i], kv.at[0, d + 1, i], kz_s.at[0, d, i], kz_r.at[d + 1, i], {"seq": right}).start()

    def key_left(d, i):
        at = lax.rem(S - d, S)
        remote(kv.at[0, at, i], kv.at[0, S - d - 1, i], kz_s.at[1, d, i], kz_r.at[S - d - 1, i], {"seq": left}).start()

    def key_across(j):
        remote(kv.at[0, j], kv.at[1, j], ks_s.at[j], ks_r.at[j], {"sub": other}).start()

    def own_w(d):
        def send(at, rows, sub):
            ds = pl.ds(pl.multiple_of(at, 16), rows)
            remote(wbuf.at[0, ds], wbuf.at[1, ds], wz_s.at[0, 0, sub], w_r.at[1, sub], {"seq": right}).start()
            remote(wbuf.at[0, ds], wbuf.at[S - 1, ds], wz_s.at[1, 0, sub], w_r.at[S - 1, sub], {"seq": left}).start()

        @pl.when(d < pieces)
        def _():
            send(first_at + d * (part // pieces), part // pieces, 0)

        @pl.when(d >= pieces)
        def _():
            send(part + (d - pieces) * (second_rows // pieces), second_rows // pieces, 1)

    def w_right(d, rows, sub):
        remote(wbuf.at[d, rows], wbuf.at[d + 1, rows], wz_s.at[0, d, sub], w_r.at[d + 1, sub], {"seq": right}).start()

    def w_left(d, rows, sub):
        remote(
            wbuf.at[S - d, rows], wbuf.at[S - d - 1, rows], wz_s.at[1, d, sub], w_r.at[S - d - 1, sub], {"seq": left}
        ).start()

    def w_pair(j):
        if use_y:
            remote(wbuf.at[j, first], wbuf.at[j, first], wy_s.at[j], w_r.at[j, 2], {"groups": partner}).start()

    def w_pair_got(j):
        if use_y:
            got(wbuf.at[j, third], w_r.at[j, 2])

    lane = lax.broadcasted_iota(jnp.int32, (8, T), 1)
    own = (s * C + c) * 2
    position = jnp.where(lane < hb, half_ref[own] * hb + lane, half_ref[own + 1] * hb + lane - hb)
    limit = jnp.zeros((8, T), jnp.int32)
    start = jnp.int32(0)
    for f in range(frame_ref.shape[0]):
        length = frame_ref[f]
        limit = limit + jnp.where(start <= position, length, 0)
        start = start + length
    limit = jnp.broadcast_to(limit[0:1], (T, T))
    row = lax.broadcasted_iota(jnp.int32, (T, T), 0)
    col = lax.broadcasted_iota(jnp.int32, (T, T), 1)
    eye = jnp.where(row == col, 1.0, 0.0).astype(jnp.bfloat16)
    vaug[:, HEAD_WIDTH:] = jnp.ones((vaug.shape[0], HEAD_WIDTH), jnp.bfloat16)

    def place(at, which, j):
        block = (lax.rem(s - j + S, S) * C + (c if which == 0 else other)) * 2
        place_at = jnp.where(row < hb, half_ref[block] * hb + row, half_ref[block + 1] * hb + row - hb)
        hidden = jnp.where(place_at < limit, 0.0, MASKED).astype(jnp.bfloat16)
        kaug[at * T : (at + 1) * T, :HEAD_WIDTH] = kv[which, j, 0]
        kaug[at * T : (at + 1) * T, HEAD_WIDTH:] = hidden
        vaug[at * T : (at + 1) * T, :HEAD_WIDTH] = kv[which, j, 1]

    def attend(slots, opening=False):
        for at, j in enumerate(slots):
            place(2 * at, 0, j)
            got(kv.at[1, j], ks_r.at[j])
            place(2 * at + 1, 1, j)
        count = 2 * len(slots) * T

        def rows_of(i, carry):
            rows = pl.ds(pl.multiple_of(i * ROW_TILE, ROW_TILE), ROW_TILE)
            scores = lax.dot_general(
                qaug[rows], kaug[:count], (((1,), (1,)), ((), ())), preferred_element_type=jnp.float32
            )
            top = jnp.max(scores, axis=1, keepdims=True)
            if opening:
                new = jnp.broadcast_to(top, (ROW_TILE, HEAD_WIDTH))
            else:
                old = m_buf[rows]
                new = jnp.maximum(old, top)
            m_buf[rows] = new
            weights = jnp.exp2((scores - jnp.concatenate([new] * (count // HEAD_WIDTH), axis=1)) * SCALE_LOG2)
            product = jnp.dot(weights.astype(jnp.bfloat16), vaug[:count], preferred_element_type=jnp.float32)
            if opening:
                acc[rows] = product
            else:
                fade = jnp.exp2((old - new) * SCALE_LOG2)
                acc[rows] = acc[rows] * jnp.concatenate([fade, fade], axis=1) + product
            return carry

        lax.fori_loop(0, heads * T // ROW_TILE, rows_of, 0)

    pl.semaphore_wait(barrier, len(peers))
    ins[0].wait()
    key_right(0, 0)
    key_left(0, 0)
    ins[1].wait()
    key_right(0, 1)
    key_left(0, 1)
    key_across(0)
    ins[3].wait()
    own_w(0)
    ins[2].wait()
    for i in range(heads):
        qaug[i * T : (i + 1) * T, :HEAD_WIDTH] = q_buf[:, i * HEAD_WIDTH : (i + 1) * HEAD_WIDTH]
        qaug[i * T : (i + 1) * T, HEAD_WIDTH:] = eye

    def key_round(d, last):
        for i in range(2):
            got(kv.at[0, d, i], kz_r.at[d, i])
            if not last or i == 0:
                key_right(d, i)
            got(kv.at[0, S - d, i], kz_r.at[S - d, i])
            if not last or i == 1:
                key_left(d, i)
        key_across(d)
        key_across(S - d)
        own_w(d)

    key_round(1, half == 2)
    attend([0], opening=True)

    def key_step(d, carry):
        key_round(d, False)
        attend([d - 1, S - d + 1])
        return carry

    lax.fori_loop(2, half - 1, key_step, 0)
    if half > 2:
        key_round(half - 1, True)
        attend([half - 2, S - half + 2])
    got(kv.at[0, half, 0], kz_r.at[half, 0])
    got(kv.at[0, half, 1], kz_r.at[half, 1])
    key_across(half)
    attend([half - 1, S - half + 1])

    def w_first(d, last):
        got(wbuf.at[d, first], w_r.at[d, 0])
        w_right(d, first, 0)
        w_pair(d)
        got(wbuf.at[S - d, first], w_r.at[S - d, 0])
        if not last:
            w_left(d, first, 0)
        w_pair(S - d)

    def w_second(d, last):
        got(wbuf.at[d, second], w_r.at[d, 1])
        if not last:
            w_right(d, second, 1)
        got(wbuf.at[S - d, second], w_r.at[S - d, 1])
        w_left(d, second, 1)

    w_first(1, half == 2)
    attend([half])
    w_second(1, half == 2)
    for i in range(heads):
        rows = slice(i * T, (i + 1) * T)
        cols = slice(i * HEAD_WIDTH, (i + 1) * HEAD_WIDTH)
        attf[0, :, cols] = (acc[rows, :HEAD_WIDTH] / acc[rows, HEAD_WIDTH:]).astype(jnp.bfloat16)
    across = remote(attf.at[0], attf.at[1], a_s, a_r, {"sub": other})
    across.start()
    att_copy = pltpu.make_async_copy(attf.at[0], att_hbm, io_sem.at[6])
    att_copy.start()

    def route(j):
        block = lax.rem(s - j + S, S)
        return block // per, lax.rem(block, per) * C + c

    def own_route(j, to, tile):
        return remote(c_out.at[j, 0], c_in.at[h, tile], c_s.at[j, 0], c_r.at[h, tile], {"heads": to})

    def project(slots):
        both = jnp.concatenate([attf[0], attf[1]], axis=0)
        weights = jnp.concatenate([wbuf[j] for j in slots], axis=1)
        terms = jnp.dot(both, weights, preferred_element_type=jnp.float32).astype(jnp.bfloat16)
        for i, j in enumerate(slots):
            for t in range(2):
                c_out[j, t] = terms[t * T : (t + 1) * T, i * T : (i + 1) * T]
        for j in slots:
            to, tile = route(j)
            remote(
                c_out.at[j, 1], c_in.at[h, tile], c_s.at[j, 1], c_r.at[h, tile], {"heads": to, "sub": other}
            ).start()

            @pl.when(to != h)
            def _():
                own_route(j, to, tile).start()

            @pl.when(to == h)
            def _():
                pltpu.make_async_copy(c_out.at[j, 0], c_in.at[h, tile], c_r.at[h, tile]).start()

    def w_step(d, carry):
        w_first(d, False)
        w_pair_got(d - 1)
        w_pair_got(S - d + 1)
        project([d - 1, S - d + 1])
        w_second(d, False)
        return carry

    if half > 2:
        w_first(2, half == 3)
        across.wait()
        project([0])
        w_second(2, half == 3)
        w_pair_got(1)
        w_pair_got(S - 1)
        project([1, S - 1])
        lax.fori_loop(3, half - 1, w_step, 0)
        w_first(half - 1, True)
        w_pair_got(half - 2)
        w_pair_got(S - half + 2)
        project([half - 2, S - half + 2])
        w_second(half - 1, True)
    else:
        across.wait()
        project([0])
    got(wbuf.at[half, first], w_r.at[half, 0])
    w_pair(half)
    w_pair_got(half - 1)
    w_pair_got(S - half + 1)
    project([half - 1, S - half + 1])
    got(wbuf.at[half, second], w_r.at[half, 1])
    w_pair_got(half)
    project([half])

    ins[4].wait()
    ins[5].wait()

    energy = jnp.zeros((T, 1), jnp.float32)
    tiles = c_in.shape[1]
    for t in range(tiles):
        cols = slice(t * T, (t + 1) * T)
        total = res_buf[:, cols].astype(jnp.float32)
        for p in range(H):
            got(c_in.at[p, t], c_r.at[p, t])
        summed = c_in[0, t].astype(jnp.float32)
        for p in range(1, H):
            summed = summed + c_in[p, t].astype(jnp.float32)
        state = (total + summed).astype(jnp.bfloat16)
        hid_buf[:, cols] = state
        wide = state.astype(jnp.float32)
        energy = energy + jnp.sum(wide * wide, axis=1, keepdims=True)
    e_out[...] = jnp.transpose(jnp.broadcast_to(energy, (T, T)))[:8]
    for i in range(1, H):
        to = lax.rem(h + i, H)
        remote(e_out, e_in.at[h], e_s.at[i], e_r.at[h], {"heads": to}).start()
    hid_copy = pltpu.make_async_copy(hid_buf, hid_hbm, io_sem.at[7])
    hid_copy.start()
    everyone = e_out[...]
    for i in range(1, H):
        of = lax.rem(h + i, H)
        got(e_in.at[of], e_r.at[of])
        everyone = everyone + e_in[of]
    mean = jnp.transpose(jnp.broadcast_to(everyone[0:1], (T, T))) * (1.0 / (T * tiles * H))
    factor = lax.rsqrt(mean + 1e-6)
    for t in range(tiles):
        cols = slice(t * T, (t + 1) * T)
        norm_buf[:, cols] = (hid_buf[:, cols].astype(jnp.float32) * factor * gain_buf[:, cols]).astype(jnp.bfloat16)
    norm_copy = pltpu.make_async_copy(norm_buf, norm_hbm, io_sem.at[8])
    norm_copy.start()

    def drain_keys(d, carry):
        for i in range(2):
            for way in range(2):
                sent(kv.at[0, 0, i], kz_s.at[way, d, i])
        return carry

    lax.fori_loop(0, half - 1, drain_keys, 0)
    sent(kv.at[0, 0, 0], kz_s.at[0, half - 1, 0])
    sent(kv.at[0, 0, 1], kz_s.at[1, half - 1, 1])

    def drain_w(d, carry):
        for way in range(2):
            sent(wbuf.at[0, first], wz_s.at[way, d, 0])
            sent(wbuf.at[0, second], wz_s.at[way, d, 1])
        return carry

    lax.fori_loop(0, half - 1, drain_w, 0)
    sent(wbuf.at[0, first], wz_s.at[0, half - 1, 0])
    sent(wbuf.at[0, second], wz_s.at[1, half - 1, 1])

    def drain_slots(j, carry):
        sent(kv.at[0, 0], ks_s.at[j])
        sent(c_out.at[0, 1], c_s.at[j, 1])
        to, tile = route(j)

        @pl.when(to != h)
        def _():
            sent(c_out.at[0, 0], c_s.at[j, 0])

        if use_y:

            @pl.when(j > 0)
            def _():
                sent(wbuf.at[0, first], wy_s.at[j])

        return carry

    lax.fori_loop(0, S, drain_slots, 0)
    for i in range(1, H):
        sent(e_out, e_s.at[i])
    att_copy.wait()
    hid_copy.wait()
    norm_copy.wait()


def shards(sizes, queries, keys, values, half_order, frame_lengths, out_proj, residual_in, norm_gain):
    G, S, H, C = sizes
    T, width = queries.shape
    K, cols = out_proj.shape
    tiles = residual_in.shape[1] // cols
    heads = width // HEAD_WIDTH
    bf16, f32, dma = jnp.bfloat16, jnp.float32, pltpu.SemaphoreType.DMA
    anywhere = pl.BlockSpec(memory_space=pl.ANY)
    smem = pl.BlockSpec(memory_space=pltpu.SMEM)
    return pl.pallas_call(
        functools.partial(fused, sizes),
        out_shape=(
            jax.ShapeDtypeStruct(queries.shape, bf16),
            jax.ShapeDtypeStruct(residual_in.shape, bf16),
            jax.ShapeDtypeStruct(residual_in.shape, bf16),
        ),
        in_specs=[smem, smem] + [anywhere] * 6,
        out_specs=(anywhere,) * 3,
        scratch_shapes=[
            pltpu.VMEM((T, width), bf16),
            pltpu.VMEM((heads * T, 2 * HEAD_WIDTH), bf16),
            pltpu.VMEM((2, S, 2, T, HEAD_WIDTH), bf16),
            pltpu.VMEM((4 * T, 2 * HEAD_WIDTH), bf16),
            pltpu.VMEM((4 * T, 2 * HEAD_WIDTH), bf16),
            pltpu.VMEM((heads * T, HEAD_WIDTH), f32),
            pltpu.VMEM((heads * T, 2 * HEAD_WIDTH), f32),
            pltpu.VMEM((2, T, width), bf16),
            pltpu.VMEM((S, K, cols), bf16),
            pltpu.VMEM((S, 2, T, cols), bf16),
            pltpu.VMEM((H, tiles, T, cols), bf16),
            pltpu.VMEM(residual_in.shape, bf16),
            pltpu.VMEM((1, residual_in.shape[1]), f32),
            pltpu.VMEM(residual_in.shape, bf16),
            pltpu.VMEM(residual_in.shape, bf16),
            pltpu.VMEM((8, T), f32),
            pltpu.VMEM((H, 8, T), f32),
            dma((9,)),
            dma((2, S // 2, 2)),
            dma((S, 2)),
            dma((S,)),
            dma((S,)),
            dma((2, S // 2, 2)),
            dma((S, 3)),
            dma((S,)),
            dma((S, 2)),
            dma((H, tiles)),
            dma(()),
            dma(()),
            dma((H,)),
            dma((H,)),
        ],
        compiler_params=pltpu.CompilerParams(collective_id=0, has_side_effects=True),
    )(half_order, frame_lengths, queries, keys, values, out_proj, residual_in, norm_gain.reshape(1, -1))


def solution(mesh):
    sizes = tuple(mesh.shape[a] for a in ("groups", "seq", "heads", "sub"))
    rows = P(("groups", "seq", "sub"), "heads")
    in_specs = (rows, rows, rows, P("groups"), P("groups"), P("heads", ("seq", "sub")), rows, P("heads"))
    return jax.shard_map(
        functools.partial(shards, sizes), mesh=mesh, in_specs=in_specs, out_specs=(rows,) * 3, check_vma=False
    )
```

time: 272 us -> 140 us (0.51)
  waiting for transfers between devices: 186 us -> 0 us
  Pallas kernels: 0 us -> 135 us
  blocking collectives: 43.8 us -> 0 us
  between operations: 15.5 us -> 0.65 us
  other arithmetic: 13.1 us -> 0 us
  matrix products: 12.9 us -> 0 us
    all_gather x2 -> x0, waiting for transfers between devices: 185 us -> none  [the longest x1 103 us: side_by_side(): lax.all_gather(both, axis, axis=dim, tiled=True)]
    pallas_call x0 -> x1, Pallas kernels: none -> 135 us  [shards(): pl.pallas_call(functools.partial(fused, sizes), out_shape=(jax.ShapeDtype...]
    all_to_all x2 -> x0, blocking collectives: 43.8 us -> none  [the longest x1 34.8 us: summed_on_arrival(): lax.all_to_all(split_up(value, dim, devices), axis, 0, 0, tiled=True)]
    dot_general x3 -> x0, matrix products: 12.9 us -> none  [the longest x1 4.64 us: shards(): jnp.dot(attended, lax.all_gather(out_proj, ('seq', 'sub'), axis=1, tiled=...]
    reduce_sum x7 -> x0, other arithmetic: 6.68 us -> none  [the longest x1 4.02 us: absorb_piece(): denominator = jnp.sum(weights, axis=-1)]
    unnamed x9 -> x7, local copies, waits for them, and re-layouts: 0.07 us -> 3.31 us
  transfers between devices with their start and end apart: 2 -> 0, of which waited for: 2 -> 0; matrix products, arithmetic and copies ran while one was open for 7% -> 0% of each run, Pallas kernels for 0% -> 0%
where the time goes in v1:
time: 140 us; the launch traced here: 139 us
  Pallas kernels  135 us (96%)
  local copies, waits for them, and re-layouts  3.31 us (2%)
    pallas_call x1, Pallas kernels, shards(): pl.pallas_call(functools.partial(fused, sizes), out_shape=(jax.ShapeDtype...  135 us
    unnamed x7, local copies, waits for them, and re-layouts  3.31 us

profile of v1, /device:TPU:65, one launch (start us, length us, event | category | flops | bytes accessed | tf_op | source)
XLA Modules:
  0.0 139.5 jit_solution(9111260293841532889)
XLA Ops:
  0.6 135.5 %shard_map.103 = (bf16[128,1024]{1,0:T(8,128)(2,1)}, bf16[128,512]{1,0:T(8,128)(2,1)}, bf16[128,512]{1,0:T(8,128)(2,1)}) custom-call(s32[64]{0:T(128)} %half_ref.1, s32[32]{0:T(128)} %frame_ref.1, bf16[128,1024]{1,0:T(8,128)(2,1)} %q_hbm.1, bf16[128,128]{1,0:T(8,128)(2,1)} %k_hbm.1, bf16[128,128]{1,0:T(8,128)(2,1)} %v_hbm.1, bf16[1024,128]{1,0:T(8,128)(2,1)} %w_hbm.1, ...), custom_call_target="tpu_custom_call" | custom-call | tf_op jit(solution)/shard_map/pallas_call | solution.py:441
  136.1 0.0 copy-start.1
  136.1 1.7 %copy.14 = bf16[128,1024]{1,0:T(8,128)(2,1)} copy(bf16[128,1024]{1,0:T(8,128)(2,1)} %get-tuple-element.6) | data formatting | bytes 524288
  137.9 0.0 copy-done.1
  137.9 0.0 copy-start
  137.9 0.7 copy.15
  138.5 0.3 copy-done
  138.8 0.7 copy.16
Async XLA Ops:
  136.1 1.7 %copy-start.1 = (bf16[128,512]{1,0:T(8,128)(2,1)S(1)}, bf16[128,512]{1,0:T(8,128)(2,1)}, u32[]{:S(2)}) copy-start(bf16[128,512]{1,0:T(8,128)(2,1)} %get-tuple-element.7) | copy-start | bytes 393220
  137.9 1.0 copy-start

commit v2 on v1

v2 whole, which is shorter than its diff:
```python
import functools

import jax
import jax.numpy as jnp
from jax import lax
from jax.experimental import pallas as pl
from jax.experimental.pallas import tpu as pltpu
from jax.sharding import PartitionSpec as P

HEAD_WIDTH = 128
MASKED = -1e30
SCALE_LOG2 = HEAD_WIDTH ** (-0.5) * 1.4426950408889634
MESH = pl.DeviceIdType.MESH
ROW_TILE = 512
LAG = 3
Y_ROWS = 5


def fused(
    sizes,
    half_ref,
    frame_ref,
    q_hbm,
    k_hbm,
    v_hbm,
    w_hbm,
    res_hbm,
    gain_hbm,
    att_hbm,
    hid_hbm,
    norm_hbm,
    q_buf,
    qaug,
    kv,
    kaug,
    vaug,
    m_buf,
    acc,
    attf,
    wbuf,
    c_out,
    c_in,
    res_buf,
    gain_buf,
    hid_buf,
    norm_buf,
    e_out,
    e_in,
    io_sem,
    line_sem,
    ring_sem,
    kz_s,
    kz_r,
    kd_s,
    ks_s,
    ks_r,
    wz_s,
    w_r,
    wd_s,
    wy_s,
    c_s,
    c_r,
    a_s,
    a_r,
    e_s,
    e_r,
):
    G, S, H, C = sizes
    use_y = G % 2 == 0
    half = S // 2
    lag = min(LAG, half - 1)
    per = S // H
    T = q_buf.shape[0]
    K = wbuf.shape[1]
    heads = q_buf.shape[1] // HEAD_WIDTH
    hb = T // 2
    g, s, h, c = (lax.axis_index(a) for a in ("groups", "seq", "heads", "sub"))
    right, left = lax.rem(s + 1, S), lax.rem(s + S - 1, S)
    h_up, h_down = lax.rem(h + 1, H), lax.rem(h + H - 1, H)
    other = 1 - c
    both, either = jnp.logical_and, jnp.logical_or

    ins = [
        pltpu.make_async_copy(k_hbm, kv.at[0, s, 0], io_sem.at[0]),
        pltpu.make_async_copy(v_hbm, kv.at[0, s, 1], io_sem.at[1]),
        pltpu.make_async_copy(q_hbm, q_buf, io_sem.at[2]),
        pltpu.make_async_copy(w_hbm, wbuf.at[s], io_sem.at[3]),
        pltpu.make_async_copy(res_hbm, res_buf, io_sem.at[4]),
        pltpu.make_async_copy(gain_hbm, gain_buf, io_sem.at[5]),
    ]
    for copy in ins:
        copy.start()

    barrier = pltpu.get_barrier_semaphore()

    def signal(sem, device):
        pl.semaphore_signal(sem, inc=1, device_id=device, device_id_type=MESH)

    signal(barrier, {"sub": other})
    signal(barrier, {"heads": h_up})
    signal(barrier, {"heads": h_down})
    greeted = 3
    if use_y:
        parity = lax.rem(g, 2)
        partner = g + 1 - 2 * parity
        signal(barrier, {"groups": partner})
        greeted = 4

    @pl.when(s > 0)
    def _():
        signal(barrier, {"seq": s - 1})

    @pl.when(s < S - 1)
    def _():
        signal(barrier, {"seq": s + 1})

    if use_y:
        part = K * Y_ROWS // 16
        first = pl.ds(pl.multiple_of(parity * (K - part), 16), part)
        second = pl.ds(part, K - 2 * part)
        third = pl.ds(pl.multiple_of((1 - parity) * (K - part), 16), part)
    else:
        part = K // 2
        first = pl.ds(0, part)
        second = pl.ds(part, K - part)
        third = None

    def remote(src, dst, send, recv, device):
        return pltpu.make_async_remote_copy(
            src_ref=src, dst_ref=dst, send_sem=send, recv_sem=recv, device_id=device, device_id_type=MESH
        )

    def got(ref, sem):
        remote(ref, ref, a_s, sem, {"sub": other}).wait_recv()

    def sent(ref, sem):
        remote(ref, ref, sem, a_r, {"sub": other}).wait_send()

    def left_needs(j):
        return either(both(s > 0, both(j >= s, j - s < half)), left - j > half)

    def right_needs(j):
        return both(s < S - 1, either(both(j <= s, s - j < half), j - s - 1 > half))

    def key_send(j, i, way):
        to = right if way else left
        remote(kv.at[0, j, i], kv.at[0, j, i], kz_s.at[way, j, i], kz_r.at[j, i], {"seq": to}).start()

    def key_direct(i):
        remote(kv.at[0, s, i], kv.at[0, s, i], kd_s.at[i], kz_r.at[s, i], {"seq": 0}).start()

    def key_across(j):
        remote(kv.at[0, j], kv.at[1, j], ks_s.at[j], ks_r.at[j], {"sub": other}).start()

    def w_send(j, i, way):
        rows = second if i else first
        to = right if way else left
        remote(wbuf.at[j, rows], wbuf.at[j, rows], wz_s.at[way, j, i], w_r.at[j, i], {"seq": to}).start()

    def w_direct(i):
        rows = second if i else first
        remote(wbuf.at[s, rows], wbuf.at[s, rows], wd_s.at[i], w_r.at[s, i], {"seq": 0}).start()

    lane = lax.broadcasted_iota(jnp.int32, (8, T), 1)
    own = (s * C + c) * 2
    position = jnp.where(lane < hb, half_ref[own] * hb + lane, half_ref[own + 1] * hb + lane - hb)
    limit = jnp.zeros((8, T), jnp.int32)
    start = jnp.int32(0)
    for f in range(frame_ref.shape[0]):
        length = frame_ref[f]
        limit = limit + jnp.where(start <= position, length, 0)
        start = start + length
    limit = jnp.broadcast_to(limit[0:1], (T, T))
    row = lax.broadcasted_iota(jnp.int32, (T, T), 0)
    col = lax.broadcasted_iota(jnp.int32, (T, T), 1)
    eye = jnp.where(row == col, 1.0, 0.0).astype(jnp.bfloat16)
    vaug[:, HEAD_WIDTH:] = jnp.ones((vaug.shape[0], HEAD_WIDTH), jnp.bfloat16)

    def place(at, which, j):
        block = (j * C + (c if which == 0 else other)) * 2
        place_at = jnp.where(row < hb, half_ref[block] * hb + row, half_ref[block + 1] * hb + row - hb)
        hidden = jnp.where(place_at < limit, 0.0, MASKED).astype(jnp.bfloat16)
        kaug[at * T : (at + 1) * T, :HEAD_WIDTH] = kv[which, j, 0]
        kaug[at * T : (at + 1) * T, HEAD_WIDTH:] = hidden
        vaug[at * T : (at + 1) * T, :HEAD_WIDTH] = kv[which, j, 1]

    def attend(j, opening=False):
        place(0, 0, j)
        got(kv.at[1, j], ks_r.at[j])
        place(1, 1, j)
        tile = min(ROW_TILE, heads * T)

        def rows_of(i, carry):
            rows = pl.ds(pl.multiple_of(i * tile, tile), tile)
            scores = lax.dot_general(
                qaug[rows], kaug[...], (((1,), (1,)), ((), ())), preferred_element_type=jnp.float32
            )
            top = jnp.max(scores, axis=1, keepdims=True)
            if opening:
                new = jnp.broadcast_to(top, (tile, HEAD_WIDTH))
            else:
                old = m_buf[rows]
                new = jnp.maximum(old, top)
            m_buf[rows] = new
            weights = jnp.exp2((scores - jnp.concatenate([new, new], axis=1)) * SCALE_LOG2)
            product = jnp.dot(weights.astype(jnp.bfloat16), vaug[...], preferred_element_type=jnp.float32)
            if opening:
                acc[rows] = product
            else:
                fade = jnp.exp2((old - new) * SCALE_LOG2)
                acc[rows] = acc[rows] * jnp.concatenate([fade, fade], axis=1) + product
            return carry

        lax.fori_loop(0, heads * T // tile, rows_of, 0)

    pl.semaphore_wait(
        barrier, greeted + jnp.where(s > 0, 1, 0).astype(jnp.int32) + jnp.where(s < S - 1, 1, 0).astype(jnp.int32)
    )

    @pl.when(s > 0)
    def _():
        pl.semaphore_wait(line_sem, 1)

    @pl.when(s < S - 1)
    def _():
        signal(line_sem, {"seq": s + 1})

    def own_keys(i):
        @pl.when(s > 0)
        def _():
            key_send(s, i, 0)

        @pl.when(s < S - 1)
        def _():
            key_send(s, i, 1)

        @pl.when(s > half)
        def _():
            key_direct(i)

    def own_w(i):
        @pl.when(s > 0)
        def _():
            w_send(s, i, 0)

        @pl.when(s < S - 1)
        def _():
            w_send(s, i, 1)

        @pl.when(s > half)
        def _():
            w_direct(i)

    ins[0].wait()
    own_keys(0)
    ins[1].wait()
    own_keys(1)
    key_across(s)
    ins[3].wait()
    own_w(0)
    own_w(1)

    for r in range(H // 2):
        signal(ring_sem.at[0, r], {"heads": h_up})
        signal(ring_sem.at[1, r], {"heads": h_down})
        pl.semaphore_wait(ring_sem.at[0, r], 1)
        pl.semaphore_wait(ring_sem.at[1, r], 1)

    ins[2].wait()
    for i in range(heads):
        qaug[i * T : (i + 1) * T, :HEAD_WIDTH] = q_buf[:, i * HEAD_WIDTH : (i + 1) * HEAD_WIDTH]
        qaug[i * T : (i + 1) * T, HEAD_WIDTH:] = eye

    def key_take(j, onward):
        for i in range(2):
            got(kv.at[0, j, i], kz_r.at[j, i])
            onward(j, i)
        key_across(j)

    def w_take(j, onward):
        got(wbuf.at[j, first], w_r.at[j, 0])
        onward(j, 0)
        if use_y:
            remote(wbuf.at[j, first], wbuf.at[j, first], wy_s.at[j], w_r.at[j, 2], {"groups": partner}).start()
        got(wbuf.at[j, second], w_r.at[j, 1])
        onward(j, 1)

    def guarded(condition, send, way):
        def onward(j, i):
            @pl.when(condition(j))
            def _():
                send(j, i, way)

        return onward

    def lines(p, act):
        @pl.when(s + p < S)
        def _():
            act(s + p, 0)

        @pl.when(s - p >= 0)
        def _():
            act(s - p, 1)

    def key_line(p):
        go = (
            guarded(lambda j: both(s > 0, p < half), key_send, 0),
            guarded(lambda j: both(s < S - 1, p < half), key_send, 1),
        )
        lines(p, lambda j, way: key_take(j, go[way]))

    def w_line(p, late):
        if late:
            up = guarded(lambda j: either(both(s > 0, p < half), both(s == 0, j < S - 1 - half)), w_send, 0)
        else:
            up = guarded(lambda j: both(s > 0, p < half), w_send, 0)
        go = (up, guarded(lambda j: both(s < S - 1, p < half), w_send, 1))
        lines(p, lambda j, way: w_take(j, go[way]))

    def wraps(k, act):
        @pl.when(s + half + k < S)
        def _():
            act(s + half + k, 1)

        @pl.when(k <= s - half)
        def _():
            act(k - 1, 0)

    def key_wrap(k):
        go = (
            guarded(lambda j: s - 1 - j > half, key_send, 0),
            guarded(lambda j: j - s - 1 > half, key_send, 1),
        )
        wraps(k, lambda j, way: key_take(j, go[way]))

    def w_wrap(k):
        go = (
            guarded(lambda j: s - 1 - j > half, w_send, 0),
            guarded(lambda j: j - s - 1 > half, w_send, 1),
        )
        wraps(k, lambda j, way: w_take(j, go[way]))

    def attend_line(p):
        lines(p, lambda j, way: attend(j))

    key_line(1)
    attend(s, opening=True)

    def line_step(p, carry):
        key_line(p)
        attend_line(p - 1)

        @pl.when(p > lag)
        def _():
            w_line(p - lag, False)

        return carry

    lax.fori_loop(2, half + 1, line_step, 0)
    attend_line(half)

    def wrap_step(k, carry):
        key_wrap(k)
        wraps(k, lambda j, way: attend(j))
        return carry

    lax.fori_loop(1, half, wrap_step, 0)

    @pl.when(s == 0)
    def _():
        def keys_round(j, carry):
            key_send(j, 0, 0)
            key_send(j, 1, 0)
            return carry

        lax.fori_loop(0, S - 1 - half, keys_round, 0)

        def w_round(j, carry):
            w_send(j, 0, 0)
            w_send(j, 1, 0)
            return carry

        lax.fori_loop(0, min(S - 1 - half, half - lag + 1), w_round, 0)

    for i in range(heads):
        rows = slice(i * T, (i + 1) * T)
        cols = slice(i * HEAD_WIDTH, (i + 1) * HEAD_WIDTH)
        attf[0, :, cols] = (acc[rows, :HEAD_WIDTH] / acc[rows, HEAD_WIDTH:]).astype(jnp.bfloat16)
    across = remote(attf.at[0], attf.at[1], a_s, a_r, {"sub": other})
    across.start()
    att_copy = pltpu.make_async_copy(attf.at[0], att_hbm, io_sem.at[6])
    att_copy.start()

    def route(j):
        return j // per, lax.rem(j, per) * C + c

    def own_route(j, to, tile):
        return remote(c_out.at[j, 0], c_in.at[h, tile], c_s.at[j, 0], c_r.at[h, tile], {"heads": to})

    def project(j):
        if use_y:

            @pl.when(j != s)
            def _():
                got(wbuf.at[j, third], w_r.at[j, 2])

        rows = jnp.concatenate([attf[0], attf[1]], axis=0)
        terms = jnp.dot(rows, wbuf[j], preferred_element_type=jnp.float32).astype(jnp.bfloat16)
        for t in range(2):
            c_out[j, t] = terms[t * T : (t + 1) * T]
        to, tile = route(j)
        remote(
            c_out.at[j, 1], c_in.at[h, tile], c_s.at[j, 1], c_r.at[h, tile], {"heads": to, "sub": other}
        ).start()

        @pl.when(to != h)
        def _():
            own_route(j, to, tile).start()

        @pl.when(to == h)
        def _():
            pltpu.make_async_copy(c_out.at[j, 0], c_in.at[h, tile], c_r.at[h, tile]).start()

    def project_line(p):
        lines(p, lambda j, way: project(j))

    across.wait()
    project(s)

    def early_step(p, carry):
        project_line(p)
        return carry

    lax.fori_loop(1, half - lag, early_step, 0)

    def late_step(p, carry):
        w_line(p, True)
        project_line(p - 1)
        return carry

    if lag < half - 1:
        lax.fori_loop(half - lag + 1, half + 1, late_step, 0)
        project_line(half)
    else:
        lax.fori_loop(2, half + 1, late_step, 0)
        project_line(half)

    def wrap_late(k, carry):
        w_wrap(k)
        wraps(k, lambda j, way: project(j))
        return carry

    lax.fori_loop(1, half, wrap_late, 0)

    ins[4].wait()
    ins[5].wait()

    energy = jnp.zeros((T, 1), jnp.float32)
    tiles = c_in.shape[1]
    for t in range(tiles):
        cols = slice(t * T, (t + 1) * T)
        total = res_buf[:, cols].astype(jnp.float32)
        for p in range(H):
            got(c_in.at[p, t], c_r.at[p, t])
        summed = c_in[0, t].astype(jnp.float32)
        for p in range(1, H):
            summed = summed + c_in[p, t].astype(jnp.float32)
        state = (total + summed).astype(jnp.bfloat16)
        hid_buf[:, cols] = state
        wide = state.astype(jnp.float32)
        energy = energy + jnp.sum(wide * wide, axis=1, keepdims=True)
    e_out[...] = jnp.transpose(jnp.broadcast_to(energy, (T, T)))[:8]
    for i in range(1, H):
        to = lax.rem(h + i, H)
        remote(e_out, e_in.at[h], e_s.at[i], e_r.at[h], {"heads": to}).start()
    hid_copy = pltpu.make_async_copy(hid_buf, hid_hbm, io_sem.at[7])
    hid_copy.start()
    everyone = e_out[...]
    for i in range(1, H):
        of = lax.rem(h + i, H)
        got(e_in.at[of], e_r.at[of])
        everyone = everyone + e_in[of]
    mean = jnp.transpose(jnp.broadcast_to(everyone[0:1], (T, T))) * (1.0 / (T * tiles * H))
    factor = lax.rsqrt(mean + 1e-6)
    for t in range(tiles):
        cols = slice(t * T, (t + 1) * T)
        norm_buf[:, cols] = (hid_buf[:, cols].astype(jnp.float32) * factor * gain_buf[:, cols]).astype(jnp.bfloat16)
    norm_copy = pltpu.make_async_copy(norm_buf, norm_hbm, io_sem.at[8])
    norm_copy.start()

    def drain(j, carry):
        for way, needs in enumerate((left_needs, right_needs)):

            @pl.when(needs(j))
            def _(way=way):
                for i in range(2):
                    sent(kv.at[0, 0, i], kz_s.at[way, j, i])
                sent(wbuf.at[0, first], wz_s.at[way, j, 0])
                sent(wbuf.at[0, second], wz_s.at[way, j, 1])

        sent(kv.at[0, 0], ks_s.at[j])
        sent(c_out.at[0, 1], c_s.at[j, 1])
        to, tile = route(j)

        @pl.when(to != h)
        def _():
            sent(c_out.at[0, 0], c_s.at[j, 0])

        if use_y:

            @pl.when(j != s)
            def _():
                sent(wbuf.at[0, first], wy_s.at[j])

        return carry

    lax.fori_loop(0, S, drain, 0)

    @pl.when(s > half)
    def _():
        for i in range(2):
            sent(kv.at[0, 0, i], kd_s.at[i])
        sent(wbuf.at[0, first], wd_s.at[0])
        sent(wbuf.at[0, second], wd_s.at[1])

    for i in range(1, H):
        sent(e_out, e_s.at[i])
    att_copy.wait()
    hid_copy.wait()
    norm_copy.wait()


def shards(sizes, queries, keys, values, half_order, frame_lengths, out_proj, residual_in, norm_gain):
    G, S, H, C = sizes
    T, width = queries.shape
    K, cols = out_proj.shape
    tiles = residual_in.shape[1] // cols
    heads = width // HEAD_WIDTH
    bf16, f32, dma = jnp.bfloat16, jnp.float32, pltpu.SemaphoreType.DMA
    anywhere = pl.BlockSpec(memory_space=pl.ANY)
    smem = pl.BlockSpec(memory_space=pltpu.SMEM)
    return pl.pallas_call(
        functools.partial(fused, sizes),
        out_shape=(
            jax.ShapeDtypeStruct(queries.shape, bf16),
            jax.ShapeDtypeStruct(residual_in.shape, bf16),
            jax.ShapeDtypeStruct(residual_in.shape, bf16),
        ),
        in_specs=[smem, smem] + [anywhere] * 6,
        out_specs=(anywhere,) * 3,
        scratch_shapes=[
            pltpu.VMEM((T, width), bf16),
            pltpu.VMEM((heads * T, 2 * HEAD_WIDTH), bf16),
            pltpu.VMEM((2, S, 2, T, HEAD_WIDTH), bf16),
            pltpu.VMEM((2 * T, 2 * HEAD_WIDTH), bf16),
            pltpu.VMEM((2 * T, 2 * HEAD_WIDTH), bf16),
            pltpu.VMEM((heads * T, HEAD_WIDTH), f32),
            pltpu.VMEM((heads * T, 2 * HEAD_WIDTH), f32),
            pltpu.VMEM((2, T, width), bf16),
            pltpu.VMEM((S, K, cols), bf16),
            pltpu.VMEM((S, 2, T, cols), bf16),
            pltpu.VMEM((H, tiles, T, cols), bf16),
            pltpu.VMEM(residual_in.shape, bf16),
            pltpu.VMEM((1, residual_in.shape[1]), f32),
            pltpu.VMEM(residual_in.shape, bf16),
            pltpu.VMEM(residual_in.shape, bf16),
            pltpu.VMEM((8, T), f32),
            pltpu.VMEM((H, 8, T), f32),
            dma((9,)),
            pltpu.SemaphoreType.REGULAR,
            pltpu.SemaphoreType.REGULAR((2, H // 2)),
            dma((2, S, 2)),
            dma((S, 2)),
            dma((2,)),
            dma((S,)),
            dma((S,)),
            dma((2, S, 2)),
            dma((S, 3)),
            dma((2,)),
            dma((S,)),
            dma((S, 2)),
            dma((H, tiles)),
            dma(()),
            dma(()),
            dma((H,)),
            dma((H,)),
        ],
        compiler_params=pltpu.CompilerParams(collective_id=0, has_side_effects=True),
    )(half_order, frame_lengths, queries, keys, values, out_proj, residual_in, norm_gain.reshape(1, -1))


def solution(mesh):
    sizes = tuple(mesh.shape[a] for a in ("groups", "seq", "heads", "sub"))
    rows = P(("groups", "seq", "sub"), "heads")
    in_specs = (rows, rows, rows, P("groups"), P("groups"), P("heads", ("seq", "sub")), rows, P("heads"))
    return jax.shard_map(
        functools.partial(shards, sizes), mesh=mesh, in_specs=in_specs, out_specs=(rows,) * 3, check_vma=False
    )
```

time: 140 us -> 177 us (1.26)
  the two profiles are of different devices: /device:TPU:65 before, /device:TPU:832 now
where the time goes in v2:
time: 177 us
  Pallas kernels  173 us (98%)
  local copies, waits for them, and re-layouts  3.31 us (2%)
    pallas_call x1, Pallas kernels, shards(): pl.pallas_call(functools.partial(fused, sizes), out_shape=(jax.ShapeDtype...  173 us

profile of v2, /device:TPU:832, one launch (start us, length us, event | category | flops | bytes accessed | tf_op | source)
XLA Modules:
  0.0 176.8 jit_solution(8411429208507059904)
XLA Ops:
  0.6 172.9 %shard_map.103 = (bf16[128,1024]{1,0:T(8,128)(2,1)}, bf16[128,512]{1,0:T(8,128)(2,1)}, bf16[128,512]{1,0:T(8,128)(2,1)}) custom-call(s32[64]{0:T(128)} %half_ref.1, s32[32]{0:T(128)} %frame_ref.1, bf16[128,1024]{1,0:T(8,128)(2,1)} %q_hbm.1, bf16[128,128]{1,0:T(8,128)(2,1)} %k_hbm.1, bf16[128,128]{1,0:T(8,128)(2,1)} %v_hbm.1, bf16[1024,128]{1,0:T(8,128)(2,1)} %w_hbm.1, ...), custom_call_target="tpu_custom_call" | custom-call | tf_op jit(solution)/shard_map/pallas_call | solution.py:542
  173.5 0.0 copy-start.1
  173.5 1.7 copy.14
  175.2 0.0 copy-done.1
  175.2 0.0 copy-start
  175.2 0.7 copy.15
  175.9 0.3 copy-done
  176.2 0.7 copy.16
Async XLA Ops:
  173.5 1.7 copy-start.1
  175.2 1.0 copy-start

commit v3 on v1

--- a/solution.py
+++ b/solution.py
@@ -12,6 +12,8 @@
 SCALE_LOG2 = HEAD_WIDTH ** (-0.5) * 1.4426950408889634
 MESH = pl.DeviceIdType.MESH
 ROW_TILE = 256
+Y_ROWS = 7
+LAG = 4
 
 
 def fused(
@@ -23,10 +25,9 @@
     v_hbm,
     w_hbm,
     res_hbm,
-    gain_hbm,
     att_hbm,
     hid_hbm,
-    norm_hbm,
+    sum_hbm,
     q_buf,
     qaug,
     kv,
@@ -39,12 +40,12 @@
     c_out,
     c_in,
     res_buf,
-    gain_buf,
     hid_buf,
-    norm_buf,
     e_out,
     e_in,
+    e_sum,
     io_sem,
+    ring_sem,
     kz_s,
     kz_r,
     ks_s,
@@ -62,6 +63,7 @@
     G, S, H, C = sizes
     use_y = G % 2 == 0
     half = S // 2
+    lag = max(1, half * LAG // 8)
     per = S // H
     T = q_buf.shape[0]
     K = wbuf.shape[1]
@@ -77,7 +79,6 @@
         pltpu.make_async_copy(q_hbm, q_buf, io_sem.at[2]),
         pltpu.make_async_copy(w_hbm, wbuf.at[0], io_sem.at[3]),
         pltpu.make_async_copy(res_hbm, res_buf, io_sem.at[4]),
-        pltpu.make_async_copy(gain_hbm, gain_buf, io_sem.at[5]),
     ]
     for copy in ins:
         copy.start()
@@ -88,15 +89,13 @@
         parity = lax.rem(g, 2)
         partner = g + 1 - 2 * parity
         peers.append({"groups": partner})
-    for i in range(1, H):
-        to = lax.rem(h + i, H)
-        peers.append({"heads": to})
-        peers.append({"heads": to, "sub": other})
+    h_up, h_down = lax.rem(h + 1, H), lax.rem(h + H - 1, H)
+    peers += [{"heads": h_up}, {"heads": h_down}]
     for peer in peers:
         pl.semaphore_signal(barrier, inc=1, device_id=peer, device_id_type=MESH)
 
     if use_y:
-        part = K * 5 // 16
+        part = K * Y_ROWS // 16
         first = pl.ds(pl.multiple_of(parity * (K - part), 16), part)
         second = pl.ds(part, K - 2 * part)
         third = pl.ds(pl.multiple_of((1 - parity) * (K - part), 16), part)
@@ -108,7 +107,7 @@
         third = None
         first_at = 0
     second_rows = K - 2 * part if use_y else K - part
-    pieces = half // 2
+    pieces = max(1, half // 4)
 
     def remote(src, dst, send, recv, device):
         return pltpu.make_async_remote_copy(
@@ -141,7 +140,7 @@
         def _():
             send(first_at + d * (part // pieces), part // pieces, 0)
 
-        @pl.when(d >= pieces)
+        @pl.when(jnp.logical_and(d >= pieces, d < 2 * pieces))
         def _():
             send(part + (d - pieces) * (second_rows // pieces), second_rows // pieces, 1)
 
@@ -184,21 +183,25 @@
         kaug[at * T : (at + 1) * T, HEAD_WIDTH:] = hidden
         vaug[at * T : (at + 1) * T, :HEAD_WIDTH] = kv[which, j, 1]
 
-    def attend(slots, opening=False):
+    tile = min(ROW_TILE, heads * T)
+
+    def prepare(slots):
         for at, j in enumerate(slots):
             place(2 * at, 0, j)
             got(kv.at[1, j], ks_r.at[j])
             place(2 * at + 1, 1, j)
+
+    def attend_rows(slots, first_tile, last_tile, opening=False):
         count = 2 * len(slots) * T
 
-        def rows_of(i, carry):
-            rows = pl.ds(pl.multiple_of(i * ROW_TILE, ROW_TILE), ROW_TILE)
+        for i in range(first_tile, last_tile):
+            rows = slice(i * tile, (i + 1) * tile)
             scores = lax.dot_general(
                 qaug[rows], kaug[:count], (((1,), (1,)), ((), ())), preferred_element_type=jnp.float32
             )
             top = jnp.max(scores, axis=1, keepdims=True)
             if opening:
-                new = jnp.broadcast_to(top, (ROW_TILE, HEAD_WIDTH))
+                new = jnp.broadcast_to(top, (tile, HEAD_WIDTH))
             else:
                 old = m_buf[rows]
                 new = jnp.maximum(old, top)
@@ -210,9 +213,26 @@
             else:
                 fade = jnp.exp2((old - new) * SCALE_LOG2)
                 acc[rows] = acc[rows] * jnp.concatenate([fade, fade], axis=1) + product
-            return carry
-
-        lax.fori_loop(0, heads * T // ROW_TILE, rows_of, 0)
+
+    row_tiles = heads * T // tile
+    mid_tile = row_tiles // 2
+
+    def attend(slots, opening=False, between=None):
+        prepare(slots)
+        attend_rows(slots, 0, mid_tile, opening)
+        if between is not None:
+            between()
+        attend_rows(slots, mid_tile, row_tiles, opening)
+
+    rounds = H // 2
+
+    def ring_signal(r):
+        pl.semaphore_signal(ring_sem.at[0, r], inc=1, device_id={"heads": h_up}, device_id_type=MESH)
+        pl.semaphore_signal(ring_sem.at[1, r], inc=1, device_id={"heads": h_down}, device_id_type=MESH)
+
+    def ring_wait(r):
+        pl.semaphore_wait(ring_sem.at[0, r], 1)
+        pl.semaphore_wait(ring_sem.at[1, r], 1)
 
     pl.semaphore_wait(barrier, len(peers))
     ins[0].wait()
@@ -224,6 +244,7 @@
     key_across(0)
     ins[3].wait()
     own_w(0)
+    ring_signal(0)
     ins[2].wait()
     for i in range(heads):
         qaug[i * T : (i + 1) * T, :HEAD_WIDTH] = q_buf[:, i * HEAD_WIDTH : (i + 1) * HEAD_WIDTH]
@@ -241,24 +262,7 @@
         key_across(S - d)
         own_w(d)
 
-    key_round(1, half == 2)
-    attend([0], opening=True)
-
-    def key_step(d, carry):
-        key_round(d, False)
-        attend([d - 1, S - d + 1])
-        return carry
-
-    lax.fori_loop(2, half - 1, key_step, 0)
-    if half > 2:
-        key_round(half - 1, True)
-        attend([half - 2, S - half + 2])
-    got(kv.at[0, half, 0], kz_r.at[half, 0])
-    got(kv.at[0, half, 1], kz_r.at[half, 1])
-    key_across(half)
-    attend([half - 1, S - half + 1])
-
-    def w_first(d, last):
+    def w_first(d, last=False):
         got(wbuf.at[d, first], w_r.at[d, 0])
         w_right(d, first, 0)
         w_pair(d)
@@ -267,31 +271,36 @@
             w_left(d, first, 0)
         w_pair(S - d)
 
-    def w_second(d, last):
+    def w_second(d, last=False):
         got(wbuf.at[d, second], w_r.at[d, 1])
         if not last:
             w_right(d, second, 1)
         got(wbuf.at[S - d, second], w_r.at[S - d, 1])
         w_left(d, second, 1)
 
-    w_first(1, half == 2)
-    attend([half])
-    w_second(1, half == 2)
-    for i in range(heads):
-        rows = slice(i * T, (i + 1) * T)
-        cols = slice(i * HEAD_WIDTH, (i + 1) * HEAD_WIDTH)
-        attf[0, :, cols] = (acc[rows, :HEAD_WIDTH] / acc[rows, HEAD_WIDTH:]).astype(jnp.bfloat16)
+    def finish():
+        for i in range(heads):
+            rows = slice(i * T, (i + 1) * T)
+            cols = slice(i * HEAD_WIDTH, (i + 1) * HEAD_WIDTH)
+            attf[0, :, cols] = (acc[rows, :HEAD_WIDTH] / acc[rows, HEAD_WIDTH:]).astype(jnp.bfloat16)
+
     across = remote(attf.at[0], attf.at[1], a_s, a_r, {"sub": other})
-    across.start()
     att_copy = pltpu.make_async_copy(attf.at[0], att_hbm, io_sem.at[6])
-    att_copy.start()
 
     def route(j):
         block = lax.rem(s - j + S, S)
-        return block // per, lax.rem(block, per) * C + c
-
-    def own_route(j, to, tile):
-        return remote(c_out.at[j, 0], c_in.at[h, tile], c_s.at[j, 0], c_r.at[h, tile], {"heads": to})
+        to = block // per
+        return to, lax.rem(block, per), lax.rem(to - h + H, H)
+
+    def deliver(j):
+        to, turn, away = route(j)
+        tile = turn * C + c
+        remote(
+            c_out.at[j, 0], c_in.at[away, tile], c_s.at[j, 0], c_r.at[away, tile], {"heads": to}
+        ).start()
+        remote(
+            c_out.at[j, 1], c_in.at[away, tile], c_s.at[j, 1], c_r.at[away, tile], {"heads": to, "sub": other}
+        ).start()
 
     def project(slots):
         both = jnp.concatenate([attf[0], attf[1]], axis=0)
@@ -300,56 +309,115 @@
         for i, j in enumerate(slots):
             for t in range(2):
                 c_out[j, t] = terms[t * T : (t + 1) * T, i * T : (i + 1) * T]
-        for j in slots:
-            to, tile = route(j)
-            remote(
-                c_out.at[j, 1], c_in.at[h, tile], c_s.at[j, 1], c_r.at[h, tile], {"heads": to, "sub": other}
-            ).start()
-
-            @pl.when(to != h)
+
+    def send_sums(nearest, furthest):
+        def owner(i, carry):
+            for turn in range(per):
+                block = lax.rem(h + i, H) * per + turn
+                j = lax.rem(s - block + S, S)
+                near = jnp.logical_and(j >= nearest, j <= furthest)
+                beyond = jnp.logical_and(S - j >= nearest, S - j <= furthest)
+
+                @pl.when(jnp.logical_or(near, beyond))
+                def _(j=j, turn=turn):
+                    @pl.when(i > 0)
+                    def _():
+                        deliver(j)
+
+                    @pl.when(i == 0)
+                    def _():
+                        tile = turn * C + c
+                        pltpu.make_async_copy(c_out.at[j, 0], c_in.at[0, tile], c_r.at[0, tile]).start()
+                        remote(
+                            c_out.at[j, 1], c_in.at[0, tile], c_s.at[j, 1], c_r.at[0, tile], {"sub": other}
+                        ).start()
+
+            return carry
+
+        lax.fori_loop(0, H, owner, 0)
+
+    key_round(1, half == 2)
+    attend([0], opening=True)
+
+    def key_step(d, carry):
+        @pl.when(d - 2 < rounds)
+        def _():
+            ring_wait(d - 2)
+
+        @pl.when(d - 1 < rounds)
+        def _():
+            ring_signal(d - 1)
+
+        key_round(d, False)
+
+        def between():
+            @pl.when(d > lag)
             def _():
-                own_route(j, to, tile).start()
-
-            @pl.when(to == h)
-            def _():
-                pltpu.make_async_copy(c_out.at[j, 0], c_in.at[h, tile], c_r.at[h, tile]).start()
-
-    def w_step(d, carry):
-        w_first(d, False)
-        w_pair_got(d - 1)
-        w_pair_got(S - d + 1)
-        project([d - 1, S - d + 1])
-        w_second(d, False)
+                w_first(d - lag)
+
+        attend([d - 1, S - d + 1], between=between)
+
+        @pl.when(d > lag)
+        def _():
+            w_second(d - lag)
+
         return carry
 
     if half > 2:
-        w_first(2, half == 3)
-        across.wait()
-        project([0])
-        w_second(2, half == 3)
-        w_pair_got(1)
-        w_pair_got(S - 1)
-        project([1, S - 1])
-        lax.fori_loop(3, half - 1, w_step, 0)
-        w_first(half - 1, True)
-        w_pair_got(half - 2)
-        w_pair_got(S - half + 2)
-        project([half - 2, S - half + 2])
-        w_second(half - 1, True)
-    else:
-        across.wait()
-        project([0])
+        lax.fori_loop(2, half - 1, key_step, 0)
+        key_round(half - 1, True)
+        attend([half - 2, S - half + 2], between=(lambda: w_first(half - 1 - lag)) if half - 1 > lag else None)
+        if half - 1 > lag:
+            w_second(half - 1 - lag)
+    for r in range(max(0, half - 3), rounds):
+        ring_wait(r)
+        if r + 1 < rounds:
+            ring_signal(r + 1)
+    got(kv.at[0, half, 0], kz_r.at[half, 0])
+    got(kv.at[0, half, 1], kz_r.at[half, 1])
+    key_across(half)
+    at = half - lag
+    attend([half - 1, S - half + 1], between=lambda: w_first(at, at == half - 1))
+    w_second(at, at == half - 1)
+
+    def closing():
+        attend([half])
+        finish()
+        across.start()
+        att_copy.start()
+
+    groups = [[0]] + [[d, S - d] for d in range(1, half)] + [[half]]
+    done = 0
+
+    def catch_up(upto):
+        nonlocal done
+        before = done
+        while done < upto:
+            for j in groups[done]:
+                if j:
+                    w_pair_got(j)
+            project(groups[done])
+            done += 1
+        if done > before:
+            send_sums(before, done - 1)
+
+    todo = [closing, lambda: (across.wait(), catch_up(max(1, half - lag)))]
+    for d in range(half - lag + 1, half):
+        w_first(d, d == half - 1)
+        if todo:
+            todo.pop(0)()
+        else:
+            catch_up(d - 1)
+        w_second(d, d == half - 1)
     got(wbuf.at[half, first], w_r.at[half, 0])
     w_pair(half)
-    w_pair_got(half - 1)
-    w_pair_got(S - half + 1)
-    project([half - 1, S - half + 1])
+    while todo:
+        todo.pop(0)()
+    catch_up(half)
     got(wbuf.at[half, second], w_r.at[half, 1])
-    w_pair_got(half)
-    project([half])
+    catch_up(half + 1)
 
     ins[4].wait()
-    ins[5].wait()
 
     energy = jnp.zeros((T, 1), jnp.float32)
     tiles = c_in.shape[1]
@@ -371,62 +439,83 @@
         remote(e_out, e_in.at[h], e_s.at[i], e_r.at[h], {"heads": to}).start()
     hid_copy = pltpu.make_async_copy(hid_buf, hid_hbm, io_sem.at[7])
     hid_copy.start()
+    def drain_keys(d, carry):
+        for i in range(2):
+            for way in range(2):
+                sent(kv.at[0, 0, i], kz_s.at[way, d, i])
+        return carry
+
+    lax.fori_loop(0, half - 1, drain_keys, 0)
+    sent(kv.at[0, 0, 0], kz_s.at[0, half - 1, 0])
+    sent(kv.at[0, 0, 1], kz_s.at[1, half - 1, 1])
+
+    def drain_w(d, carry):
+        for way in range(2):
+            sent(wbuf.at[0, first], wz_s.at[way, d, 0])
+            sent(wbuf.at[0, second], wz_s.at[way, d, 1])
+        return carry
+
+    lax.fori_loop(0, half - 1, drain_w, 0)
+    sent(wbuf.at[0, first], wz_s.at[0, half - 1, 0])
+    sent(wbuf.at[0, second], wz_s.at[1, half - 1, 1])
+
+    def drain_slots(j, carry):
+        sent(kv.at[0, 0], ks_s.at[j])
+        away = route(j)[2]
+        sent(c_out.at[0, 1], c_s.at[j, 1])
+
+        @pl.when(away > 0)
+        def _():
+            sent(c_out.at[0, 0], c_s.at[j, 0])
+
+        if use_y:
+
+            @pl.when(j > 0)
+            def _():
+                sent(wbuf.at[0, first], wy_s.at[j])
+
+        return carry
+
+    lax.fori_loop(0, S, drain_slots, 0)
     everyone = e_out[...]
     for i in range(1, H):
         of = lax.rem(h + i, H)
         got(e_in.at[of], e_r.at[of])
         everyone = everyone + e_in[of]
-    mean = jnp.transpose(jnp.broadcast_to(everyone[0:1], (T, T))) * (1.0 / (T * tiles * H))
-    factor = lax.rsqrt(mean + 1e-6)
-    for t in range(tiles):
-        cols = slice(t * T, (t + 1) * T)
-        norm_buf[:, cols] = (hid_buf[:, cols].astype(jnp.float32) * factor * gain_buf[:, cols]).astype(jnp.bfloat16)
-    norm_copy = pltpu.make_async_copy(norm_buf, norm_hbm, io_sem.at[8])
-    norm_copy.start()
-
-    def drain_keys(d, carry):
-        for i in range(2):
-            for way in range(2):
-                sent(kv.at[0, 0, i], kz_s.at[way, d, i])
-        return carry
-
-    lax.fori_loop(0, half - 1, drain_keys, 0)
-    sent(kv.at[0, 0, 0], kz_s.at[0, half - 1, 0])
-    sent(kv.at[0, 0, 1], kz_s.at[1, half - 1, 1])
-
-    def drain_w(d, carry):
-        for way in range(2):
-            sent(wbuf.at[0, first], wz_s.at[way, d, 0])
-            sent(wbuf.at[0, second], wz_s.at[way, d, 1])
-        return carry
-
-    lax.fori_loop(0, half - 1, drain_w, 0)
-    sent(wbuf.at[0, first], wz_s.at[0, half - 1, 0])
-    sent(wbuf.at[0, second], wz_s.at[1, half - 1, 1])
-
-    def drain_slots(j, carry):
-        sent(kv.at[0, 0], ks_s.at[j])
-        sent(c_out.at[0, 1], c_s.at[j, 1])
-        to, tile = route(j)
-
-        @pl.when(to != h)
-        def _():
-            sent(c_out.at[0, 0], c_s.at[j, 0])
-
-        if use_y:
-
-            @pl.when(j > 0)
-            def _():
-                sent(wbuf.at[0, first], wy_s.at[j])
-
-        return carry
-
-    lax.fori_loop(0, S, drain_slots, 0)
+    e_sum[...] = everyone
+    sum_copy = pltpu.make_async_copy(e_sum, sum_hbm, io_sem.at[8])
+    sum_copy.start()
     for i in range(1, H):
         sent(e_out, e_s.at[i])
     att_copy.wait()
     hid_copy.wait()
-    norm_copy.wait()
+    sum_copy.wait()
+
+
+def norm(width, sum_hbm, gain_hbm, att_hbm, hid_hbm, att_out, hid_out, norm_out, e_sum, gain, att, hid, normed, sems):
+    T, cols = hid.shape
+    pairs = ((att_hbm, att), (hid_hbm, hid), (sum_hbm, e_sum), (gain_hbm, gain))
+    ins = [pltpu.make_async_copy(a, b, sems.at[i]) for i, (a, b) in enumerate(pairs)]
+    for copy in ins:
+        copy.start()
+    outs = [
+        pltpu.make_async_copy(a, b, sems.at[4 + i])
+        for i, (a, b) in enumerate(((att, att_out), (hid, hid_out), (normed, norm_out)))
+    ]
+    ins[0].wait()
+    outs[0].start()
+    ins[1].wait()
+    outs[1].start()
+    ins[2].wait()
+    ins[3].wait()
+    mean = jnp.transpose(jnp.broadcast_to(e_sum[0:1], (T, T))) * (1.0 / width)
+    factor = lax.rsqrt(mean + 1e-6)
+    for t in range(cols // T):
+        at = slice(t * T, (t + 1) * T)
+        normed[:, at] = (hid[:, at].astype(jnp.float32) * factor * gain[:, at]).astype(jnp.bfloat16)
+    outs[2].start()
+    for copy in outs:
+        copy.wait()
 
 
 def shards(sizes, queries, keys, values, half_order, frame_lengths, out_proj, residual_in, norm_gain):
@@ -438,14 +527,14 @@
     bf16, f32, dma = jnp.bfloat16, jnp.float32, pltpu.SemaphoreType.DMA
     anywhere = pl.BlockSpec(memory_space=pl.ANY)
     smem = pl.BlockSpec(memory_space=pltpu.SMEM)
-    return pl.pallas_call(
+    attended, hidden, sums = pl.pallas_call(
         functools.partial(fused, sizes),
         out_shape=(
             jax.ShapeDtypeStruct(queries.shape, bf16),
             jax.ShapeDtypeStruct(residual_in.shape, bf16),
-            jax.ShapeDtypeStruct(residual_in.shape, bf16),
+            jax.ShapeDtypeStruct((8, T), f32),
         ),
-        in_specs=[smem, smem] + [anywhere] * 6,
+        in_specs=[smem, smem] + [anywhere] * 5,
         out_specs=(anywhere,) * 3,
         scratch_shapes=[
             pltpu.VMEM((T, width), bf16),
@@ -460,12 +549,12 @@
             pltpu.VMEM((S, 2, T, cols), bf16),
             pltpu.VMEM((H, tiles, T, cols), bf16),
             pltpu.VMEM(residual_in.shape, bf16),
-            pltpu.VMEM((1, residual_in.shape[1]), f32),
-            pltpu.VMEM(residual_in.shape, bf16),
             pltpu.VMEM(residual_in.shape, bf16),
             pltpu.VMEM((8, T), f32),
             pltpu.VMEM((H, 8, T), f32),
+            pltpu.VMEM((8, T), f32),
             dma((9,)),
+            pltpu.SemaphoreType.REGULAR((2, H // 2)),
             dma((2, S // 2, 2)),
             dma((S, 2)),
             dma((S,)),
@@ -481,7 +570,25 @@
             dma((H,)),
         ],
         compiler_params=pltpu.CompilerParams(collective_id=0, has_side_effects=True),
-    )(half_order, frame_lengths, queries, keys, values, out_proj, residual_in, norm_gain.reshape(1, -1))
+    )(half_order, frame_lengths, queries, keys, values, out_proj, residual_in)
+    return pl.pallas_call(
+        functools.partial(norm, residual_in.shape[1] * H),
+        out_shape=(
+            jax.ShapeDtypeStruct(queries.shape, bf16),
+            jax.ShapeDtypeStruct(residual_in.shape, bf16),
+            jax.ShapeDtypeStruct(residual_in.shape, bf16),
+        ),
+        in_specs=[anywhere] * 4,
+        out_specs=(anywhere,) * 3,
+        scratch_shapes=[
+            pltpu.VMEM((8, T), f32),
+            pltpu.VMEM((1, residual_in.shape[1]), f32),
+            pltpu.VMEM((T, width), bf16),
+            pltpu.VMEM(residual_in.shape, bf16),
+            pltpu.VMEM(residual_in.shape, bf16),
+            dma((7,)),
+        ],
+    )(sums, norm_gain.reshape(1, -1), attended, hidden)
 
 
 def solution(mesh):

time: 140 us -> 133 us (0.950)
  local copies, waits for them, and re-layouts: 3.31 us -> 0 us
  Pallas kernels: 135 us -> 132 us
    pallas_call x1, Pallas kernels: 135 us -> 131 us  [shards(): pl.pallas_call(functools.partial(fused, sizes), out_shape=(jax.ShapeDtype...]
    unnamed x7 -> x0, local copies, waits for them, and re-layouts: 3.31 us -> none
    pallas_call x0 -> x1, Pallas kernels: none -> 1.82 us  [shards(): pl.pallas_call(functools.partial(norm, residual_in.shape[1] * H), out_sha...]
where the time goes in v3:
time: 133 us
  Pallas kernels  132 us (99%)
    pallas_call x1, Pallas kernels, shards(): pl.pallas_call(functools.partial(fused, sizes), out_shape=(jax.ShapeDtype...  131 us

profile of v3, /device:TPU:65, one launch (start us, length us, event | category | flops | bytes accessed | tf_op | source)
XLA Modules:
  0.0 133.1 jit_solution(11606619490647093239)
XLA Ops:
  0.6 130.6 %shard_map.103 = (bf16[128,1024]{1,0:T(8,128)(2,1)}, bf16[128,512]{1,0:T(8,128)(2,1)}, f32[8,128]{1,0:T(8,128)}) custom-call(s32[64]{0:T(128)} %half_ref.1, s32[32]{0:T(128)} %frame_ref.1, bf16[128,1024]{1,0:T(8,128)(2,1)} %q_hbm.1, bf16[128,128]{1,0:T(8,128)(2,1)} %k_hbm.1, bf16[128,128]{1,0:T(8,128)(2,1)} %v_hbm.1, bf16[1024,128]{1,0:T(8,128)(2,1)} %w_hbm.1, ...), custom_call_target="tpu_custom_call" | custom-call | tf_op jit(solution)/shard_map/pallas_call | solution.py:530
  131.2 1.8 %shard_map.104 = (bf16[128,1024]{1,0:T(8,128)(2,1)}, bf16[128,512]{1,0:T(8,128)(2,1)}, bf16[128,512]{1,0:T(8,128)(2,1)}) custom-call(f32[8,128]{1,0:T(8,128)} %get-tuple-element.6.sum_hbm, f32[1,512]{1,0:T(1,128)} %bitcast.1, bf16[128,1024]{1,0:T(8,128)(2,1)} %get-tuple-element.7.att_hbm, bf16[128,512]{1,0:T(8,128)(2,1)} %get-tuple-element.8.hid_hbm), custom_call_target="tpu_custom_call" | custom-call | tf_op jit(solution)/shard_map/pallas_call | solution.py:574

commit v4 on v3

--- a/solution.py
+++ b/solution.py
@@ -12,7 +12,7 @@
 SCALE_LOG2 = HEAD_WIDTH ** (-0.5) * 1.4426950408889634
 MESH = pl.DeviceIdType.MESH
 ROW_TILE = 256
-Y_ROWS = 7
+Y_ROWS = 6
 LAG = 4
 
 
@@ -39,6 +39,8 @@
     wbuf,
     c_out,
     c_in,
+    m_in,
+    m_far,
     res_buf,
     hid_buf,
     e_out,
@@ -55,6 +57,8 @@
     wy_s,
     c_s,
     c_r,
+    m_r,
+    f_r,
     a_s,
     a_r,
     e_s,
@@ -65,6 +69,7 @@
     half = S // 2
     lag = max(1, half * LAG // 8)
     per = S // H
+    merging = H == 8
     T = q_buf.shape[0]
     K = wbuf.shape[1]
     heads = q_buf.shape[1] // HEAD_WIDTH
@@ -310,31 +315,61 @@
             for t in range(2):
                 c_out[j, t] = terms[t * T : (t + 1) * T, i * T : (i + 1) * T]
 
-    def send_sums(nearest, furthest):
-        def owner(i, carry):
+    def send_slot(j):
+        turn, away = route(j)[1:]
+
+        def hand(part, dst, send, recv, step):
+            remote(part, dst, send, recv, {"heads": lax.rem(h + step + H, H)}).start()
+
+        if merging:
+            direct = jnp.logical_or(away == 1, away == H - 1)
+
+            @pl.when(away == 3)
+            def _():
+                hand(c_out.at[j], m_in.at[0, turn], c_s.at[j, 0], m_r.at[0, turn], 1)
+
+            @pl.when(away == 5)
+            def _():
+                hand(c_out.at[j], m_in.at[1, turn], c_s.at[j, 0], m_r.at[1, turn], -1)
+
+            @pl.when(away == 4)
+            def _():
+                hand(c_out.at[j, 0], m_far.at[0, turn], c_s.at[j, 0], f_r.at[0, turn], 2)
+                hand(c_out.at[j, 1], m_far.at[1, turn], c_s.at[j, 1], f_r.at[1, turn], -2)
+        else:
+            direct = away > 0
+
+        @pl.when(direct)
+        def _():
+            deliver(j)
+
+        @pl.when(away == 0)
+        def _():
+            tile = turn * C + c
+            pltpu.make_async_copy(c_out.at[j, 0], c_in.at[0, tile], c_r.at[0, tile]).start()
+            remote(c_out.at[j, 1], c_in.at[0, tile], c_s.at[j, 1], c_r.at[0, tile], {"sub": other}).start()
+
+    def merge_sums(nearest, furthest):
+        if not merging:
+            return
+        for side, away in enumerate((2, 6)):
             for turn in range(per):
-                block = lax.rem(h + i, H) * per + turn
+                block = lax.rem(h + away, H) * per + turn
                 j = lax.rem(s - block + S, S)
-                near = jnp.logical_and(j >= nearest, j <= furthest)
-                beyond = jnp.logical_and(S - j >= nearest, S - j <= furthest)
-
-                @pl.when(jnp.logical_or(near, beyond))
-                def _(j=j, turn=turn):
-                    @pl.when(i > 0)
-                    def _():
-                        deliver(j)
-
-                    @pl.when(i == 0)
-                    def _():
-                        tile = turn * C + c
-                        pltpu.make_async_copy(c_out.at[j, 0], c_in.at[0, tile], c_r.at[0, tile]).start()
-                        remote(
-                            c_out.at[j, 1], c_in.at[0, tile], c_s.at[j, 1], c_r.at[0, tile], {"sub": other}
-                        ).start()
-
-            return carry
-
-        lax.fori_loop(0, H, owner, 0)
+                planes = jnp.minimum(j, S - j)
+
+                @pl.when(jnp.logical_and(planes >= nearest, planes <= furthest))
+                def _(side=side, turn=turn, j=j):
+                    got(m_in.at[side, turn], m_r.at[side, turn])
+                    got(m_far.at[side, turn], f_r.at[side, turn])
+                    near = m_in[side, turn].astype(jnp.float32)
+                    far = m_far[side, turn].astype(jnp.float32)
+                    for t in range(2):
+                        total = c_out[j, t].astype(jnp.float32) + near[t]
+                        if t == side:
+                            total = total + far
+                        c_out[j, t] = total.astype(jnp.bfloat16)
+                    deliver(j)
 
     key_round(1, half == 2)
     attend([0], opening=True)
@@ -391,15 +426,14 @@
 
     def catch_up(upto):
         nonlocal done
-        before = done
         while done < upto:
             for j in groups[done]:
                 if j:
                     w_pair_got(j)
             project(groups[done])
+            for j in groups[done]:
+                send_slot(j)
             done += 1
-        if done > before:
-            send_sums(before, done - 1)
 
     todo = [closing, lambda: (across.wait(), catch_up(max(1, half - lag)))]
     for d in range(half - lag + 1, half):
@@ -413,21 +447,25 @@
     w_pair(half)
     while todo:
         todo.pop(0)()
+    early = done - 1
     catch_up(half)
     got(wbuf.at[half, second], w_r.at[half, 1])
     catch_up(half + 1)
+    merge_sums(0, early)
+    merge_sums(early + 1, half)
 
     ins[4].wait()
 
     energy = jnp.zeros((T, 1), jnp.float32)
     tiles = c_in.shape[1]
+    senders = (0, 1, 2, 6, 7) if merging else tuple(range(H))
     for t in range(tiles):
         cols = slice(t * T, (t + 1) * T)
         total = res_buf[:, cols].astype(jnp.float32)
-        for p in range(H):
+        for p in senders:
             got(c_in.at[p, t], c_r.at[p, t])
         summed = c_in[0, t].astype(jnp.float32)
-        for p in range(1, H):
+        for p in senders[1:]:
             summed = summed + c_in[p, t].astype(jnp.float32)
         state = (total + summed).astype(jnp.bfloat16)
         hid_buf[:, cols] = state
@@ -462,11 +500,19 @@
     def drain_slots(j, carry):
         sent(kv.at[0, 0], ks_s.at[j])
         away = route(j)[2]
-        sent(c_out.at[0, 1], c_s.at[j, 1])
-
-        @pl.when(away > 0)
-        def _():
-            sent(c_out.at[0, 0], c_s.at[j, 0])
+        whole = jnp.logical_or(away == 3, away == 5) if merging else away < 0
+
+        @pl.when(whole)
+        def _():
+            sent(c_out.at[0], c_s.at[j, 0])
+
+        @pl.when(jnp.logical_not(whole))
+        def _():
+            sent(c_out.at[0, 1], c_s.at[j, 1])
+
+            @pl.when(away > 0)
+            def _():
+                sent(c_out.at[0, 0], c_s.at[j, 0])
 
         if use_y:
 
@@ -548,6 +594,8 @@
             pltpu.VMEM((S, K, cols), bf16),
             pltpu.VMEM((S, 2, T, cols), bf16),
             pltpu.VMEM((H, tiles, T, cols), bf16),
+            pltpu.VMEM((2, S // H, 2, T, cols), bf16),
+            pltpu.VMEM((2, S // H, T, cols), bf16),
             pltpu.VMEM(residual_in.shape, bf16),
             pltpu.VMEM(residual_in.shape, bf16),
             pltpu.VMEM((8, T), f32),
@@ -564,6 +612,8 @@
             dma((S,)),
             dma((S, 2)),
             dma((H, tiles)),
+            dma((2, S // H)),
+            dma((2, S // H)),
             dma(()),
             dma(()),
             dma((H,)),

time: 133 us -> 124 us (0.932)
  Pallas kernels: 132 us -> 123 us
    pallas_call x1, Pallas kernels: 131 us -> 121 us  [shards(): pl.pallas_call(functools.partial(fused, sizes), out_shape=(jax.ShapeDtype...]
where the time goes in v4:
time: 124 us
  Pallas kernels  123 us (99%)
    pallas_call x1, Pallas kernels, shards(): pl.pallas_call(functools.partial(fused, sizes), out_shape=(jax.ShapeDtype...  121 us

profile of v4, /device:TPU:65, one launch (start us, length us, event | category | flops | bytes accessed | tf_op | source)
XLA Modules:
  0.0 123.9 jit_solution(13966828150705398889)
XLA Ops:
  0.6 121.5 %shard_map.103 = (bf16[128,1024]{1,0:T(8,128)(2,1)}, bf16[128,512]{1,0:T(8,128)(2,1)}, f32[8,128]{1,0:T(8,128)}) custom-call(s32[64]{0:T(128)} %half_ref.1, s32[32]{0:T(128)} %frame_ref.1, bf16[128,1024]{1,0:T(8,128)(2,1)} %q_hbm.1, bf16[128,128]{1,0:T(8,128)(2,1)} %k_hbm.1, bf16[128,128]{1,0:T(8,128)(2,1)} %v_hbm.1, bf16[1024,128]{1,0:T(8,128)(2,1)} %w_hbm.1, ...), custom_call_target="tpu_custom_call" | custom-call | tf_op jit(solution)/shard_map/pallas_call | solution.py:576
  122.1 1.8 %shard_map.104 = (bf16[128,1024]{1,0:T(8,128)(2,1)}, bf16[128,512]{1,0:T(8,128)(2,1)}, bf16[128,512]{1,0:T(8,128)(2,1)}) custom-call(f32[8,128]{1,0:T(8,128)} %get-tuple-element.6.sum_hbm, f32[1,512]{1,0:T(1,128)} %bitcast.1, bf16[128,1024]{1,0:T(8,128)(2,1)} %get-tuple-element.7.att_hbm, bf16[128,512]{1,0:T(8,128)(2,1)} %get-tuple-element.8.hid_hbm), custom_call_target="tpu_custom_call" | custom-call | tf_op jit(solution)/shard_map/pallas_call | solution.py:624

commit v5 on v4

--- a/solution.py
+++ b/solution.py
@@ -13,7 +13,7 @@
 MESH = pl.DeviceIdType.MESH
 ROW_TILE = 256
 Y_ROWS = 6
-LAG = 4
+LAG = 2
 
 
 def fused(

time: 124 us -> 121 us (0.976)
  Pallas kernels: 123 us -> 120 us
    pallas_call x1, Pallas kernels: 121 us -> 118 us  [shards(): pl.pallas_call(functools.partial(fused, sizes), out_shape=(jax.ShapeDtype...]
where the time goes in v5:
time: 121 us
  Pallas kernels  120 us (99%)
    pallas_call x1, Pallas kernels, shards(): pl.pallas_call(functools.partial(fused, sizes), out_shape=(jax.ShapeDtype...  118 us

profile of v5, /device:TPU:65, one launch (start us, length us, event | category | flops | bytes accessed | tf_op | source)
XLA Modules:
  0.0 120.5 jit_solution(14771676122502149621)
XLA Ops:
  0.6 118.0 %shard_map.103 = (bf16[128,1024]{1,0:T(8,128)(2,1)}, bf16[128,512]{1,0:T(8,128)(2,1)}, f32[8,128]{1,0:T(8,128)}) custom-call(s32[64]{0:T(128)} %half_ref.1, s32[32]{0:T(128)} %frame_ref.1, bf16[128,1024]{1,0:T(8,128)(2,1)} %q_hbm.1, bf16[128,128]{1,0:T(8,128)(2,1)} %k_hbm.1, bf16[128,128]{1,0:T(8,128)(2,1)} %v_hbm.1, bf16[1024,128]{1,0:T(8,128)(2,1)} %w_hbm.1, ...), custom_call_target="tpu_custom_call" | custom-call | tf_op jit(solution)/shard_map/pallas_call | solution.py:576
  118.7 1.8 %shard_map.104 = (bf16[128,1024]{1,0:T(8,128)(2,1)}, bf16[128,512]{1,0:T(8,128)(2,1)}, bf16[128,512]{1,0:T(8,128)(2,1)}) custom-call(f32[8,128]{1,0:T(8,128)} %get-tuple-element.6.sum_hbm, f32[1,512]{1,0:T(1,128)} %bitcast.1, bf16[128,1024]{1,0:T(8,128)(2,1)} %get-tuple-element.7.att_hbm, bf16[128,512]{1,0:T(8,128)(2,1)} %get-tuple-element.8.hid_hbm), custom_call_target="tpu_custom_call" | custom-call | tf_op jit(solution)/shard_map/pallas_call | solution.py:624
